TPU v7x, 32 devices: a whole 2x2x4 slice. The times are simulated.
32 devices in a mesh: groups: 2 (over x), ep: 8 (over z, y), node: 2 (over core).
Axes of the slice: x: 2, y: 2, z: 4, core: 2. Of those that a mesh axis runs over, the one named last changes fastest.
Arguments:
- tokens: bfloat16 [1024, 7168], P(('groups', 'ep', 'node')), parts along dimension 0, may hold values from -6 to 6
- expert_ids: int32 [1024, 8], P(('groups', 'ep', 'node')), parts along dimension 0, may hold values from 0 to 15, all different within a row; in each aligned block of 32 rows (0 to 31, 32 to 63, ...) at most 32 rows name the same one
- gate_weights: float32 [1024, 8], P(('groups', 'ep', 'node')), parts along dimension 0, may hold values from 0.05 to 0.5
- gate_up_weight: bfloat16 [16, 7168, 512], P(('ep', 'node')), may hold values from -0.0625 to 0.0625
- down_weight: bfloat16 [16, 256, 7168], P(('ep', 'node')), may hold values from -0.375 to 0.375
Outputs:
- moe_out: bfloat16 [1024, 7168], P(('groups', 'ep', 'node')), parts along dimension 0
There are 2 independent parts, one for each index of `groups`. A program takes and returns all parts, laid end to end along the dimension named above; an argument that names none is the same for every part. Nothing has to cross between parts.
Inputs may be any that keep to these rules, and one draw needn't show every extreme that they name: `expert_ids`: each token names 8 different experts; among the 32 tokens of one device no expert is named by more than 32 of them, a bound that some block reaches.
All inputs are finite; a program needn't handle non-finite values.
Results may differ from a plain program's by a relative error of at most 0.0058.
Values may be sent and summed in bfloat16 or wider, within the bound.
No kernel may reach another device: no remote copies, remote signals or barrier semaphores. Data moves between devices by JAX's collectives and lax.ppermute only.
A program may use at most 128 MiB of HBM per device.

v0:
```python
import functools

import jax
import jax.numpy as jnp
from jax import lax
from jax.experimental import pallas as pl
from jax.experimental.pallas import tpu as pltpu
from jax.sharding import PartitionSpec as P


SUBSETS = 2
LANES = 128
ROWS = 128


def ring_order(mesh):
    at = mesh.axis_names.index("ep")
    count = mesh.devices.shape[at]
    line = [mesh.devices[tuple(i if d == at else 0 for d in range(mesh.devices.ndim))] for i in range(count)]
    places = [getattr(device, "coords", None) for device in line]
    if any(place is None for place in places):
        return list(range(count))
    varying = [d for d in range(3) if len({place[d] for place in places}) > 1]
    if len(varying) == 2:
        short, long = sorted(varying, key=lambda d: len({place[d] for place in places}))
        low = min(place[short] for place in places)
        if len({place[short] for place in places}) == 2:
            there = sorted((i for i in range(count) if places[i][short] == low), key=lambda i: places[i][long])
            back = sorted((i for i in range(count) if places[i][short] != low), key=lambda i: -places[i][long])
            return there + back
    return list(range(count))


def resident(x):
    pieces = 8
    rows = x.shape[0] // pieces

    def body(x_ref, o_ref, sems):
        copies = [
            pltpu.make_async_copy(
                x_ref.at[pl.ds(i * rows, rows)], o_ref.at[pl.ds(i * rows, rows)], sems.at[i]
            )
            for i in range(pieces)
        ]
        for copy in copies:
            copy.start()
        for copy in copies:
            copy.wait()

    return pl.pallas_call(
        body,
        out_shape=pltpu.VMEM(x.shape, x.dtype),
        in_specs=[pl.BlockSpec(memory_space=pltpu.HBM)],
        out_specs=pl.BlockSpec(memory_space=pltpu.VMEM),
        scratch_shapes=[pltpu.SemaphoreType.DMA((pieces,))],
        compiler_params=pltpu.CompilerParams(vmem_limit_bytes=1 << 20),
        cost_estimate=pl.CostEstimate(flops=500 * x.size, bytes_accessed=4 * x.size, transcendentals=0),
    )(pltpu.with_memory_space_constraint(x, pltpu.HBM))


def expert_body(width, inner, node_size, local_count, block_count, *refs):
    expert_count = node_size * local_count
    expert_total = lax.axis_size("ep") * expert_count
    blocks = refs[:block_count]
    ups = refs[block_count : block_count + expert_count]
    downs = refs[block_count + expert_count : block_count + 2 * expert_count]
    out_refs, x_ref = refs[block_count + 2 * expert_count : -1], refs[-1]
    me = lax.axis_index("ep") * node_size
    core = lax.axis_index("node")
    numbers = [
        (me + lax.rem(core + shift, node_size)) * local_count + local
        for shift in range(node_size)
        for local in range(local_count)
    ]
    row = 0
    for block in blocks:
        x_ref[row : row + block.shape[0], :] = block[...]
        row += block.shape[0]
    side = x_ref[:, width:].astype(jnp.float32)
    lane = lax.broadcasted_iota(jnp.int32, side.shape, 1)
    hidden, scales = [], []
    for e in range(expert_count):
        total = jnp.dot(x_ref[:, :width], ups[e][...], preferred_element_type=jnp.float32)
        hidden.append((jax.nn.silu(total[:, :inner]) * total[:, inner:]).astype(jnp.bfloat16))
        mine = (lane == numbers[e]) | (lane == numbers[e] + expert_total) | (lane == numbers[e] + 2 * expert_total)
        scales.append(jnp.sum(jnp.where(mine, side, 0.0), axis=1, keepdims=True))
    tile = 512 if width % 512 == 0 else LANES
    for n in range(width // tile):
        at = slice(n * tile, (n + 1) * tile)
        y = None
        for e in range(expert_count):
            part = scales[e] * jnp.dot(hidden[e], downs[e][:, at], preferred_element_type=jnp.float32)
            y = part if y is None else y + part
        row = 0
        for out in out_refs:
            out[:, at] = y[row : row + out.shape[0]].astype(out.dtype)
            row += out.shape[0]


def apply_experts(blocks, dtypes, ups, downs, node_size):
    inner, width = downs[0].shape
    rows = sum(block.shape[0] for block in blocks)
    vmem = pl.BlockSpec(memory_space=pltpu.VMEM)
    weights = [pltpu.with_memory_space_constraint(x, pltpu.VMEM) for x in (*ups, *downs)]
    inputs = [*blocks, *weights]
    return pl.pallas_call(
        functools.partial(expert_body, width, inner, node_size, len(ups) // node_size, len(blocks)),
        out_shape=[jax.ShapeDtypeStruct((b.shape[0], width), dtype) for b, dtype in zip(blocks, dtypes)],
        in_specs=[vmem] * len(inputs),
        out_specs=[vmem] * len(blocks),
        scratch_shapes=[pltpu.VMEM((rows, blocks[0].shape[1]), jnp.bfloat16)],
        compiler_params=pltpu.CompilerParams(vmem_limit_bytes=12 << 20),
        cost_estimate=pl.CostEstimate(
            flops=6 * rows * width * inner * len(ups), bytes_accessed=rows * width * 6, transcendentals=rows * inner
        ),
    )(*inputs)


def make_on_device(order, node_size):
    count = len(order)
    half_way = count // 2
    onward = [(order[i], order[(i + 1) % count]) for i in range(count)]
    backward = [(order[i], order[i - 1]) for i in range(count)]

    def on(x):
        return lax.ppermute(x, "ep", onward)

    def back(x):
        return lax.ppermute(x, "ep", backward)

    def gather(own):
        rows = own.shape[0] // 2
        left, right = own, own
        blocks = [own]
        for i in range(half_way):
            if i == half_way - 1:
                left, right = left[:rows], right[rows:]
            left = on(left)
            right = back(right)
            blocks += [left, right]
        return blocks

    def scatter(sums):
        left, right = sums[-2:]
        rows, other = left.shape[0], right.shape[0]
        for i in range(half_way):
            left = on(left)
            right = back(right)
            left, right = left.astype(jnp.float32), right.astype(jnp.float32)
            if i == 0:
                left = jnp.pad(left, ((0, other), (0, 0)))
                right = jnp.pad(right, ((rows, 0), (0, 0)))
            distance = half_way - 1 - i
            if distance:
                left = (left + sums[2 * distance]).astype(jnp.bfloat16)
                right = (right + sums[2 * distance - 1]).astype(jnp.bfloat16)
        return (sums[0] + left + right).astype(jnp.bfloat16)

    def on_device(tokens, expert_ids, gate_weights, gate_up_weight, down_weight):
        token_count, _ = tokens.shape
        local_count = gate_up_weight.shape[0]
        expert_total = count * node_size * local_count
        chosen = expert_ids[:, :, None] == jnp.arange(expert_total, dtype=jnp.int32)
        rest = jnp.sum(jnp.where(chosen, gate_weights[:, :, None], 0.0), axis=1)
        parts = []
        for _ in range(3):
            part = lax.reduce_precision(rest, 8, 7)
            rest = rest - part
            parts.append(part)
        side = jnp.concatenate(parts, axis=1).astype(jnp.bfloat16)
        side = jnp.pad(side, ((0, 0), (0, -side.shape[1] % LANES)))
        ups, downs = [], []
        for shift in range(node_size):
            up, down = gate_up_weight, down_weight
            if shift:
                ring = [(i, (i - shift) % node_size) for i in range(node_size)]
                up, down = lax.ppermute((up, down), "node", ring)
            for local in range(local_count):
                for held, weight in ((ups, up[local]), (downs, down[local])):
                    held.append(resident(weight))
        rows = token_count // SUBSETS
        gathered = []
        for s in range(SUBSETS):
            at = slice(s * rows, (s + 1) * rows)
            gathered.append(gather(jnp.concatenate([tokens[at], side[at]], axis=1)))
        outs = []
        for s in range(SUBSETS):
            blocks, sums = gathered[s], []
            dtypes = [jnp.float32] * (len(blocks) - 2) + [jnp.bfloat16] * 2
            per_call = max(1, ROWS // rows) + 1
            starts = list(range(len(blocks), 0, -per_call))
            for end in reversed(starts):
                at = slice(max(0, end - per_call), end)
                sums += apply_experts(blocks[at], dtypes[at], ups, downs, node_size)
            outs.append(scatter(sums))
        return jnp.concatenate(outs, axis=0)

    return on_device


def solution(mesh):
    placed = (
        P(("groups", "ep", "node"), None),
        P(("groups", "ep", "node"), None),
        P(("groups", "ep", "node"), None),
        P(("ep", "node"), None, None),
        P(("ep", "node"), None, None),
    )
    return jax.shard_map(
        make_on_device(ring_order(mesh), mesh.shape["node"]),
        mesh=mesh,
        in_specs=placed,
        out_specs=P(("groups", "ep", "node"), None),
        check_vma=False,
    )
```

profile of v0, /device:TPU:0, one launch (start us, length us, event | category | flops | bytes accessed | tf_op | source)
XLA Modules:
  0.0 91.3 jit_solution(6189191677172924436)
XLA Ops:
  0.5 1.1 %fusion.7 = (bf16[16,7168]{1,0:T(8,128)(2,1)S(1)}, bf16[16,7168]{1,0:T(8,128)(2,1)S(1)}) fusion(bf16[32,7168]{1,0:T(8,128)(2,1)} %param.5), kind=kLoop, calls=%fused_computation.29 | loop fusion | bytes 917504 | tf_op jit(solution)/shard_map/slice | solution.py:185
  1.6 0.7 select_reduce_fusion
  2.6 3.1 %collective-permute-start = (bf16[16,7296]{1,0:T(8,128)(2,1)S(1)}, bf16[16,7296]{1,0:T(8,128)(2,1)S(1)}, u32[]{:S(2)}, u32[]{:S(2)}) collective-permute-start(bf16[16,7296]{1,0:T(8,128)(2,1)S(1)} %pad_maximum_fusion.1.refs_0_), channel_id=1, source_target_pairs={{0,4},{4,8},{8,12},{12,14},{14,10},{10,6},{6,2},{2,0},{1,5},{5,9},... | collective-permute-start | bytes 700424 | tf_op jit(solution)/shard_map/ppermute | solution.py:126
  5.7 2.1 %collective-permute-start.18 = (bf16[16,7296]{1,0:T(8,128)(2,1)S(1)}, bf16[16,7296]{1,0:T(8,128)(2,1)S(1)}, u32[]{:S(2)}, u32[]{:S(2)}) collective-permute-start(bf16[16,7296]{1,0:T(8,128)(2,1)S(1)} %pad_maximum_fusion.2.refs_0_), channel_id=1, source_target_pairs={{0,4},{4,8},{8,12},{12,14},{14,10},{10,6},{6,2},{2,0},{1,5},{5,9},... | collective-permute-start | bytes 700424 | tf_op jit(solution)/shard_map/ppermute | solution.py:126
  7.8 4.4 %collective-permute-done.refs_1_ = bf16[16,7296]{1,0:T(8,128)(2,1)S(1)} collective-permute-done((bf16[16,7296]{1,0:T(8,128)(2,1)S(1)}, bf16[16,7296]{1,0:T(8,128)(2,1)S(1)}, u32[]{:S(2)}, u32[]{:S(2)}) %collective-permute-start) | collective-permute-done | bytes 233504 | tf_op jit(solution)/shard_map/ppermute | solution.py:126
  12.2 2.0 %collective-permute-start.19 = (bf16[16,7296]{1,0:T(8,128)(2,1)S(1)}, bf16[16,7296]{1,0:T(8,128)(2,1)S(1)}, u32[]{:S(2)}, u32[]{:S(2)}) collective-permute-start(bf16[16,7296]{1,0:T(8,128)(2,1)S(1)} %pad_maximum_fusion.2.refs_0_), channel_id=1, source_target_pairs={{0,2},{4,0},{8,4},{12,8},{14,12},{10,14},{6,10},{2,6},{1,3},{5,1},... | collective-permute-start | bytes 700424 | tf_op jit(solution)/shard_map/ppermute | solution.py:129
  14.6 2.6 %collective-permute-done.18.refs_1_ = bf16[16,7296]{1,0:T(8,128)(2,1)S(1)} collective-permute-done((bf16[16,7296]{1,0:T(8,128)(2,1)S(1)}, bf16[16,7296]{1,0:T(8,128)(2,1)S(1)}, u32[]{:S(2)}, u32[]{:S(2)}) %collective-permute-start.18) | collective-permute-done | bytes 233504 | tf_op jit(solution)/shard_map/ppermute | solution.py:126
  17.2 2.0 %collective-permute-start.3 = (bf16[16,7296]{1,0:T(8,128)(2,1)S(1)}, bf16[16,7296]{1,0:T(8,128)(2,1)S(1)}, u32[]{:S(2)}, u32[]{:S(2)}) collective-permute-start(bf16[16,7296]{1,0:T(8,128)(2,1)S(1)} %collective-permute-done.1.refs_2_), channel_id=1, source_target_pairs={{0,2},{4,0},{8,4},{12,8},{14,12},{10,14},{6,10},{2,6},{1,3},{5,1},... | collective-permute-start | bytes 700424 | tf_op jit(solution)/shard_map/ppermute | solution.py:129
  19.2 1.4 %collective-permute-start.20 = (bf16[16,7296]{1,0:T(8,128)(2,1)S(1)}, bf16[16,7296]{1,0:T(8,128)(2,1)S(1)}, u32[]{:S(2)}, u32[]{:S(2)}) collective-permute-start(bf16[16,7296]{1,0:T(8,128)(2,1)S(1)} %collective-permute-done.18.refs_1_), channel_id=1, source_target_pairs={{0,4},{4,8},{8,12},{12,14},{14,10},{10,6},{6,2},{2,0},{1,5},{5,9},... | collective-permute-start | bytes 700424 | tf_op jit(solution)/shard_map/ppermute | solution.py:126
  20.6 2.2 %collective-permute-done.2.refs_3_ = bf16[16,7296]{1,0:T(8,128)(2,1)S(1)} collective-permute-done((bf16[16,7296]{1,0:T(8,128)(2,1)S(1)}, bf16[16,7296]{1,0:T(8,128)(2,1)S(1)}, u32[]{:S(2)}, u32[]{:S(2)}) %collective-permute-start.2) | collective-permute-done | bytes 233504 | tf_op jit(solution)/shard_map/ppermute | solution.py:126
  22.8 1.6 %collective-permute-start.21 = (bf16[16,7296]{1,0:T(8,128)(2,1)S(1)}, bf16[16,7296]{1,0:T(8,128)(2,1)S(1)}, u32[]{:S(2)}, u32[]{:S(2)}) collective-permute-start(bf16[16,7296]{1,0:T(8,128)(2,1)S(1)} %collective-permute-done.19.refs_2_), channel_id=1, source_target_pairs={{0,2},{4,0},{8,4},{12,8},{14,12},{10,14},{6,10},{2,6},{1,3},{5,1},... | collective-permute-start | bytes 700424 | tf_op jit(solution)/shard_map/ppermute | solution.py:129
  24.4 1.3 %collective-permute-start.4 = (bf16[16,7296]{1,0:T(8,128)(2,1)S(1)}, bf16[16,7296]{1,0:T(8,128)(2,1)S(1)}, u32[]{:S(2)}, u32[]{:S(2)}) collective-permute-start(bf16[16,7296]{1,0:T(8,128)(2,1)S(1)} %collective-permute-done.2.refs_3_), channel_id=1, source_target_pairs={{0,4},{4,8},{8,12},{12,14},{14,10},{10,6},{6,2},{2,0},{1,5},{5,9},... | collective-permute-start | bytes 700424 | tf_op jit(solution)/shard_map/ppermute | solution.py:126
  25.6 2.2 %collective-permute-done.20.refs_3_ = bf16[16,7296]{1,0:T(8,128)(2,1)S(1)} collective-permute-done((bf16[16,7296]{1,0:T(8,128)(2,1)S(1)}, bf16[16,7296]{1,0:T(8,128)(2,1)S(1)}, u32[]{:S(2)}, u32[]{:S(2)}) %collective-permute-start.20) | collective-permute-done | bytes 233504 | tf_op jit(solution)/shard_map/ppermute | solution.py:126
  27.8 1.6 %collective-permute-start.5 = (bf16[16,7296]{1,0:T(8,128)(2,1)S(1)}, bf16[16,7296]{1,0:T(8,128)(2,1)S(1)}, u32[]{:S(2)}, u32[]{:S(2)}) collective-permute-start(bf16[16,7296]{1,0:T(8,128)(2,1)S(1)} %collective-permute-done.3.refs_4_), channel_id=1, source_target_pairs={{0,2},{4,0},{8,4},{12,8},{14,12},{10,14},{6,10},{2,6},{1,3},{5,1},... | collective-permute-start | bytes 700424 | tf_op jit(solution)/shard_map/ppermute | solution.py:129
  29.4 1.2 %collective-permute-start.22 = (bf16[16,7296]{1,0:T(8,128)(2,1)S(1)}, bf16[16,7296]{1,0:T(8,128)(2,1)S(1)}, u32[]{:S(2)}, u32[]{:S(2)}) collective-permute-start(bf16[16,7296]{1,0:T(8,128)(2,1)S(1)} %collective-permute-done.20.refs_3_), channel_id=1, source_target_pairs={{0,4},{4,8},{8,12},{12,14},{14,10},{10,6},{6,2},{2,0},{1,5},{5,9},... | collective-permute-start | bytes 700424 | tf_op jit(solution)/shard_map/ppermute | solution.py:126
  30.6 2.3 %collective-permute-done.4.refs_5_ = bf16[16,7296]{1,0:T(8,128)(2,1)S(1)} collective-permute-done((bf16[16,7296]{1,0:T(8,128)(2,1)S(1)}, bf16[16,7296]{1,0:T(8,128)(2,1)S(1)}, u32[]{:S(2)}, u32[]{:S(2)}) %collective-permute-start.4) | collective-permute-done | bytes 233504 | tf_op jit(solution)/shard_map/ppermute | solution.py:126
  32.9 1.6 %collective-permute-start.23 = (bf16[16,7296]{1,0:T(8,128)(2,1)S(1)}, bf16[16,7296]{1,0:T(8,128)(2,1)S(1)}, u32[]{:S(2)}, u32[]{:S(2)}) collective-permute-start(bf16[16,7296]{1,0:T(8,128)(2,1)S(1)} %collective-permute-done.21.refs_4_), channel_id=1, source_target_pairs={{0,2},{4,0},{8,4},{12,8},{14,12},{10,14},{6,10},{2,6},{1,3},{5,1},... | collective-permute-start | bytes 700424 | tf_op jit(solution)/shard_map/ppermute | solution.py:129
  34.5 2.1 %shard_map.57.refs_11_ = bf16[256,7168]{1,0:T(8,128)(2,1)S(1)} custom-call(bf16[256,7168]{1,0:T(8,128)(2,1)} %bitcast.5), custom_call_target="tpu_custom_call" | custom-call | flops 917504000 | bytes 7340032 | tf_op jit(solution)/shard_map/pallas_call | solution.py:50
  36.6 3.2 %shard_map.55.refs_9_ = bf16[7168,512]{1,0:T(8,128)(2,1)S(1)} custom-call(bf16[7168,512]{1,0:T(8,128)(2,1)} %bitcast.4), custom_call_target="tpu_custom_call" | custom-call | flops 1835008000 | bytes 14680064 | tf_op jit(solution)/shard_map/pallas_call | solution.py:50
  39.8 0.5 collective-permute-start.6
  40.3 1.6 %collective-permute-start.7 = (bf16[8,7296]{1,0:T(8,128)(2,1)S(1)}, bf16[8,7296]{1,0:T(8,128)(2,1)S(1)}, u32[]{:S(2)}, u32[]{:S(2)}) collective-permute-start(bf16[8,7296]{1,0:T(8,128)(2,1)S(1)} %slice.34), channel_id=1, source_target_pairs={{0,2},{4,0},{8,4},{12,8},{14,12},{10,14},{6,10},{2,6},{1,3},{5,1},... | collective-permute-start | bytes 350216 | tf_op jit(solution)/shard_map/ppermute | solution.py:129
  42.0 0.5 collective-permute-start.24
  42.5 1.6 %collective-permute-start.25 = (bf16[8,7296]{1,0:T(8,128)(2,1)S(1)}, bf16[8,7296]{1,0:T(8,128)(2,1)S(1)}, u32[]{:S(2)}, u32[]{:S(2)}) collective-permute-start(bf16[8,7296]{1,0:T(8,128)(2,1)S(1)} %slice.37), channel_id=1, source_target_pairs={{0,2},{4,0},{8,4},{12,8},{14,12},{10,14},{6,10},{2,6},{1,3},{5,1},... | collective-permute-start | bytes 350216 | tf_op jit(solution)/shard_map/ppermute | solution.py:129
  44.1 2.1 %shard_map.58.refs_12_ = bf16[256,7168]{1,0:T(8,128)(2,1)S(1)} custom-call(bf16[256,7168]{1,0:T(8,128)(2,1)} %bitcast.3.x_ref), custom_call_target="tpu_custom_call" | custom-call | flops 917504000 | bytes 7340032 | tf_op jit(solution)/shard_map/pallas_call | solution.py:50
  46.2 3.2 %shard_map.56.refs_10_ = bf16[7168,512]{1,0:T(8,128)(2,1)S(1)} custom-call(bf16[7168,512]{1,0:T(8,128)(2,1)} %bitcast.1.x_ref), custom_call_target="tpu_custom_call" | custom-call | flops 1835008000 | bytes 14680064 | tf_op jit(solution)/shard_map/pallas_call | solution.py:50
  49.4 3.3 %shard_map.59 = (f32[16,7168]{1,0:T(8,128)S(1)}, f32[16,7168]{1,0:T(8,128)S(1)}, f32[16,7168]{1,0:T(8,128)S(1)}, f32[16,7168]{1,0:T(8,128)S(1)}, f32[16,7168]{1,...) custom-call(bf16[16,7296]{1,0:T(8,128)(2,1)S(1)} %pad_maximum_fusion, ...), custom_call_target="tpu_custom_call" | custom-call | flops 2818572288 | bytes 5505024 | tf_op jit(solution)/shard_map/pallas_call | solution.py:106
  52.7 0.5 collective-permute-start.10
  53.2 1.6 %collective-permute-start.14 = (bf16[8,7168]{1,0:T(8,128)(2,1)S(1)}, bf16[8,7168]{1,0:T(8,128)(2,1)S(1)}, u32[]{:S(2)}, u32[]{:S(2)}) collective-permute-start(bf16[8,7168]{1,0:T(8,128)(2,1)S(1)} %get-tuple-element.28), channel_id=1, source_target_pairs={{0,2},{4,0},{8,4},{12,8},{14,12},{10,14},{6,10},{2,6},{1,3},{5,1},... | collective-permute-start | bytes 344072 | tf_op jit(solution)/shard_map/ppermute | solution.py:129
  54.8 3.3 %shard_map.60 = (f32[16,7168]{1,0:T(8,128)S(1)}, f32[16,7168]{1,0:T(8,128)S(1)}, f32[16,7168]{1,0:T(8,128)S(1)}, f32[16,7168]{1,0:T(8,128)S(1)}, f32[16,7168]{1,...) custom-call(bf16[16,7296]{1,0:T(8,128)(2,1)S(1)} %pad_maximum_fusion, ...), custom_call_target="tpu_custom_call" | custom-call | flops 2818572288 | bytes 5505024 | tf_op jit(solution)/shard_map/pallas_call | solution.py:106
  58.1 0.5 collective-permute-start.26
  58.6 1.6 %collective-permute-start.30 = (bf16[8,7168]{1,0:T(8,128)(2,1)S(1)}, bf16[8,7168]{1,0:T(8,128)(2,1)S(1)}, u32[]{:S(2)}, u32[]{:S(2)}) collective-permute-start(bf16[8,7168]{1,0:T(8,128)(2,1)S(1)} %get-tuple-element.37), channel_id=1, source_target_pairs={{0,2},{4,0},{8,4},{12,8},{14,12},{10,14},{6,10},{2,6},{1,3},{5,1},... | collective-permute-start | bytes 344072 | tf_op jit(solution)/shard_map/ppermute | solution.py:129
  60.7 1.6 %collective-permute-start.15 = (bf16[16,7168]{1,0:T(8,128)(2,1)S(1)}, bf16[16,7168]{1,0:T(8,128)(2,1)S(1)}, u32[]{:S(2)}, u32[]{:S(2)}) collective-permute-start(bf16[16,7168]{1,0:T(8,128)(2,1)S(1)} %add_convert_fusion.10), channel_id=1, source_target_pairs={{0,2},{4,0},{8,4},{12,8},{14,12},{10,14},{6,10},{2,6},{1,3},{5,1},... | collective-permute-start | bytes 688136 | tf_op jit(solution)/shard_map/ppermute | solution.py:129
  62.4 1.8 %collective-permute-done.26 = bf16[8,7168]{1,0:T(8,128)(2,1)S(1)} collective-permute-done((bf16[8,7168]{1,0:T(8,128)(2,1)S(1)}, bf16[8,7168]{1,0:T(8,128)(2,1)S(1)}, u32[]{:S(2)}, u32[]{:S(2)}) %collective-permute-start.26) | collective-permute-done | bytes 114720 | tf_op jit(solution)/shard_map/ppermute | solution.py:126
  64.2 0.5 collective-permute-start.27
  64.7 1.6 %collective-permute-start.31 = (bf16[16,7168]{1,0:T(8,128)(2,1)S(1)}, bf16[16,7168]{1,0:T(8,128)(2,1)S(1)}, u32[]{:S(2)}, u32[]{:S(2)}) collective-permute-start(bf16[16,7168]{1,0:T(8,128)(2,1)S(1)} %add_convert_fusion.3), channel_id=1, source_target_pairs={{0,2},{4,0},{8,4},{12,8},{14,12},{10,14},{6,10},{2,6},{1,3},{5,1},... | collective-permute-start | bytes 688136 | tf_op jit(solution)/shard_map/ppermute | solution.py:129
  66.3 2.7 %collective-permute-done.11 = bf16[16,7168]{1,0:T(8,128)(2,1)S(1)} collective-permute-done((bf16[16,7168]{1,0:T(8,128)(2,1)S(1)}, bf16[16,7168]{1,0:T(8,128)(2,1)S(1)}, u32[]{:S(2)}, u32[]{:S(2)}) %collective-permute-start.11) | collective-permute-done | bytes 229408 | tf_op jit(solution)/shard_map/ppermute | solution.py:126
  69.1 0.5 collective-permute-start.12
  69.6 1.6 %collective-permute-start.16 = (bf16[16,7168]{1,0:T(8,128)(2,1)S(1)}, bf16[16,7168]{1,0:T(8,128)(2,1)S(1)}, u32[]{:S(2)}, u32[]{:S(2)}) collective-permute-start(bf16[16,7168]{1,0:T(8,128)(2,1)S(1)} %add_convert_fusion.9), channel_id=1, source_target_pairs={{0,2},{4,0},{8,4},{12,8},{14,12},{10,14},{6,10},{2,6},{1,3},{5,1},... | collective-permute-start | bytes 688136 | tf_op jit(solution)/shard_map/ppermute | solution.py:129
  71.3 2.7 %collective-permute-done.27 = bf16[16,7168]{1,0:T(8,128)(2,1)S(1)} collective-permute-done((bf16[16,7168]{1,0:T(8,128)(2,1)S(1)}, bf16[16,7168]{1,0:T(8,128)(2,1)S(1)}, u32[]{:S(2)}, u32[]{:S(2)}) %collective-permute-start.27) | collective-permute-done | bytes 229408 | tf_op jit(solution)/shard_map/ppermute | solution.py:126
  74.5 1.6 %collective-permute-start.32 = (bf16[16,7168]{1,0:T(8,128)(2,1)S(1)}, bf16[16,7168]{1,0:T(8,128)(2,1)S(1)}, u32[]{:S(2)}, u32[]{:S(2)}) collective-permute-start(bf16[16,7168]{1,0:T(8,128)(2,1)S(1)} %add_convert_fusion.2), channel_id=1, source_target_pairs={{0,2},{4,0},{8,4},{12,8},{14,12},{10,14},{6,10},{2,6},{1,3},{5,1},... | collective-permute-start | bytes 688136 | tf_op jit(solution)/shard_map/ppermute | solution.py:129
  76.2 2.7 %collective-permute-done.12 = bf16[16,7168]{1,0:T(8,128)(2,1)S(1)} collective-permute-done((bf16[16,7168]{1,0:T(8,128)(2,1)S(1)}, bf16[16,7168]{1,0:T(8,128)(2,1)S(1)}, u32[]{:S(2)}, u32[]{:S(2)}) %collective-permute-start.12) | collective-permute-done | bytes 229408 | tf_op jit(solution)/shard_map/ppermute | solution.py:126
  79.5 1.6 %collective-permute-start.17 = (bf16[16,7168]{1,0:T(8,128)(2,1)S(1)}, bf16[16,7168]{1,0:T(8,128)(2,1)S(1)}, u32[]{:S(2)}, u32[]{:S(2)}) collective-permute-start(bf16[16,7168]{1,0:T(8,128)(2,1)S(1)} %add_convert_fusion.8), channel_id=1, source_target_pairs={{0,2},{4,0},{8,4},{12,8},{14,12},{10,14},{6,10},{2,6},{1,3},{5,1},... | collective-permute-start | bytes 688136 | tf_op jit(solution)/shard_map/ppermute | solution.py:129
  81.1 2.7 %collective-permute-done.28 = bf16[16,7168]{1,0:T(8,128)(2,1)S(1)} collective-permute-done((bf16[16,7168]{1,0:T(8,128)(2,1)S(1)}, bf16[16,7168]{1,0:T(8,128)(2,1)S(1)}, u32[]{:S(2)}, u32[]{:S(2)}) %collective-permute-start.28) | collective-permute-done | bytes 229408 | tf_op jit(solution)/shard_map/ppermute | solution.py:126
  84.4 1.6 %collective-permute-start.33 = (bf16[16,7168]{1,0:T(8,128)(2,1)S(1)}, bf16[16,7168]{1,0:T(8,128)(2,1)S(1)}, u32[]{:S(2)}, u32[]{:S(2)}) collective-permute-start(bf16[16,7168]{1,0:T(8,128)(2,1)S(1)} %add_convert_fusion.1), channel_id=1, source_target_pairs={{0,2},{4,0},{8,4},{12,8},{14,12},{10,14},{6,10},{2,6},{1,3},{5,1},... | collective-permute-start | bytes 688136 | tf_op jit(solution)/shard_map/ppermute | solution.py:129
  86.0 1.3 %collective-permute-done.13 = bf16[16,7168]{1,0:T(8,128)(2,1)S(1)} collective-permute-done((bf16[16,7168]{1,0:T(8,128)(2,1)S(1)}, bf16[16,7168]{1,0:T(8,128)(2,1)S(1)}, u32[]{:S(2)}, u32[]{:S(2)}) %collective-permute-start.13) | collective-permute-done | bytes 229408 | tf_op jit(solution)/shard_map/ppermute | solution.py:126
  87.8 2.1 %collective-permute-done.29 = bf16[16,7168]{1,0:T(8,128)(2,1)S(1)} collective-permute-done((bf16[16,7168]{1,0:T(8,128)(2,1)S(1)}, bf16[16,7168]{1,0:T(8,128)(2,1)S(1)}, u32[]{:S(2)}, u32[]{:S(2)}) %collective-permute-start.29) | collective-permute-done | bytes 229408 | tf_op jit(solution)/shard_map/ppermute | solution.py:126
  89.9 0.5 collective-permute-done.33
  90.5 0.8 pad_maximum_fusion
  (55 shorter events, 4.3 us)
Async XLA Ops:
  0.0 46.2 %collective-permute-start.8 = (bf16[1,7168,512]{2,1,0:T(8,128)(2,1)}, bf16[1,7168,512]{2,1,0:T(8,128)(2,1)}, u32[]{:S(2)}, u32[]{:S(2)}) collective-permute-start(bf16[1,7168,512]{2,1,0:T(8,128)(2,1)} %param.8), channel_id=1, source_target_pairs={{0,1},{1,0},{2,3},{3,2},{4,5},{5,4},{6,7},{7,6},{8,9},{9,8},{10,11... | collective-permute-start | bytes 22020104 | tf_op jit(solution)/shard_map/ppermute | solution.py:177
  0.5 42.0 %collective-permute-start.9 = (bf16[1,256,7168]{2,1,0:T(8,128)(2,1)}, bf16[1,256,7168]{2,1,0:T(8,128)(2,1)}, u32[]{:S(2)}, u32[]{:S(2)}) collective-permute-start(bf16[1,256,7168]{2,1,0:T(8,128)(2,1)} %param.9), channel_id=1, source_target_pairs={{0,1},{1,0},{2,3},{3,2},{4,5},{5,4},{6,7},{7,6},{8,9},{9,8},{10,11... | collective-permute-start | bytes 11010056 | tf_op jit(solution)/shard_map/ppermute | solution.py:177
  2.6 9.6 %collective-permute-start = (bf16[16,7296]{1,0:T(8,128)(2,1)S(1)}, bf16[16,7296]{1,0:T(8,128)(2,1)S(1)}, u32[]{:S(2)}, u32[]{:S(2)}) collective-permute-start(bf16[16,7296]{1,0:T(8,128)(2,1)S(1)} %pad_maximum_fusion.1.refs_0_), channel_id=1, source_target_pairs={{0,4},{4,8},{8,12},{12,14},{14,10},{10,6},{6,2},{2,0},{1,5},{5,9},... | collective-permute-start | bytes 700424 | tf_op jit(solution)/shard_map/ppermute | solution.py:126
  5.7 8.5 %collective-permute-start.1 = (bf16[16,7296]{1,0:T(8,128)(2,1)S(1)}, bf16[16,7296]{1,0:T(8,128)(2,1)S(1)}, u32[]{:S(2)}, u32[]{:S(2)}) collective-permute-start(bf16[16,7296]{1,0:T(8,128)(2,1)S(1)} %pad_maximum_fusion.1.refs_0_), channel_id=1, source_target_pairs={{0,2},{4,0},{8,4},{12,8},{14,12},{10,14},{6,10},{2,6},{1,3},{5,1},... | collective-permute-start | bytes 700424 | tf_op jit(solution)/shard_map/ppermute | solution.py:129
  5.7 11.5 %collective-permute-start.18 = (bf16[16,7296]{1,0:T(8,128)(2,1)S(1)}, bf16[16,7296]{1,0:T(8,128)(2,1)S(1)}, u32[]{:S(2)}, u32[]{:S(2)}) collective-permute-start(bf16[16,7296]{1,0:T(8,128)(2,1)S(1)} %pad_maximum_fusion.2.refs_0_), channel_id=1, source_target_pairs={{0,4},{4,8},{8,12},{12,14},{14,10},{10,6},{6,2},{2,0},{1,5},{5,9},... | collective-permute-start | bytes 700424 | tf_op jit(solution)/shard_map/ppermute | solution.py:126
  12.2 7.0 %collective-permute-start.19 = (bf16[16,7296]{1,0:T(8,128)(2,1)S(1)}, bf16[16,7296]{1,0:T(8,128)(2,1)S(1)}, u32[]{:S(2)}, u32[]{:S(2)}) collective-permute-start(bf16[16,7296]{1,0:T(8,128)(2,1)S(1)} %pad_maximum_fusion.2.refs_0_), channel_id=1, source_target_pairs={{0,2},{4,0},{8,4},{12,8},{14,12},{10,14},{6,10},{2,6},{1,3},{5,1},... | collective-permute-start | bytes 700424 | tf_op jit(solution)/shard_map/ppermute | solution.py:129
  14.2 8.6 %collective-permute-start.2 = (bf16[16,7296]{1,0:T(8,128)(2,1)S(1)}, bf16[16,7296]{1,0:T(8,128)(2,1)S(1)}, u32[]{:S(2)}, u32[]{:S(2)}) collective-permute-start(bf16[16,7296]{1,0:T(8,128)(2,1)S(1)} %collective-permute-done.refs_1_), channel_id=1, source_target_pairs={{0,4},{4,8},{8,12},{12,14},{14,10},{10,6},{6,2},{2,0},{1,5},{5,9},... | collective-permute-start | bytes 700424 | tf_op jit(solution)/shard_map/ppermute | solution.py:126
  17.2 7.2 %collective-permute-start.3 = (bf16[16,7296]{1,0:T(8,128)(2,1)S(1)}, bf16[16,7296]{1,0:T(8,128)(2,1)S(1)}, u32[]{:S(2)}, u32[]{:S(2)}) collective-permute-start(bf16[16,7296]{1,0:T(8,128)(2,1)S(1)} %collective-permute-done.1.refs_2_), channel_id=1, source_target_pairs={{0,2},{4,0},{8,4},{12,8},{14,12},{10,14},{6,10},{2,6},{1,3},{5,1},... | collective-permute-start | bytes 700424 | tf_op jit(solution)/shard_map/ppermute | solution.py:129
  19.2 8.6 %collective-permute-start.20 = (bf16[16,7296]{1,0:T(8,128)(2,1)S(1)}, bf16[16,7296]{1,0:T(8,128)(2,1)S(1)}, u32[]{:S(2)}, u32[]{:S(2)}) collective-permute-start(bf16[16,7296]{1,0:T(8,128)(2,1)S(1)} %collective-permute-done.18.refs_1_), channel_id=1, source_target_pairs={{0,4},{4,8},{8,12},{12,14},{14,10},{10,6},{6,2},{2,0},{1,5},{5,9},... | collective-permute-start | bytes 700424 | tf_op jit(solution)/shard_map/ppermute | solution.py:126
  22.8 6.6 %collective-permute-start.21 = (bf16[16,7296]{1,0:T(8,128)(2,1)S(1)}, bf16[16,7296]{1,0:T(8,128)(2,1)S(1)}, u32[]{:S(2)}, u32[]{:S(2)}) collective-permute-start(bf16[16,7296]{1,0:T(8,128)(2,1)S(1)} %collective-permute-done.19.refs_2_), channel_id=1, source_target_pairs={{0,2},{4,0},{8,4},{12,8},{14,12},{10,14},{6,10},{2,6},{1,3},{5,1},... | collective-permute-start | bytes 700424 | tf_op jit(solution)/shard_map/ppermute | solution.py:129
  24.4 8.6 %collective-permute-start.4 = (bf16[16,7296]{1,0:T(8,128)(2,1)S(1)}, bf16[16,7296]{1,0:T(8,128)(2,1)S(1)}, u32[]{:S(2)}, u32[]{:S(2)}) collective-permute-start(bf16[16,7296]{1,0:T(8,128)(2,1)S(1)} %collective-permute-done.2.refs_3_), channel_id=1, source_target_pairs={{0,4},{4,8},{8,12},{12,14},{14,10},{10,6},{6,2},{2,0},{1,5},{5,9},... | collective-permute-start | bytes 700424 | tf_op jit(solution)/shard_map/ppermute | solution.py:126
  27.8 12.0 %collective-permute-start.5 = (bf16[16,7296]{1,0:T(8,128)(2,1)S(1)}, bf16[16,7296]{1,0:T(8,128)(2,1)S(1)}, u32[]{:S(2)}, u32[]{:S(2)}) collective-permute-start(bf16[16,7296]{1,0:T(8,128)(2,1)S(1)} %collective-permute-done.3.refs_4_), channel_id=1, source_target_pairs={{0,2},{4,0},{8,4},{12,8},{14,12},{10,14},{6,10},{2,6},{1,3},{5,1},... | collective-permute-start | bytes 700424 | tf_op jit(solution)/shard_map/ppermute | solution.py:129
  29.4 10.9 %collective-permute-start.22 = (bf16[16,7296]{1,0:T(8,128)(2,1)S(1)}, bf16[16,7296]{1,0:T(8,128)(2,1)S(1)}, u32[]{:S(2)}, u32[]{:S(2)}) collective-permute-start(bf16[16,7296]{1,0:T(8,128)(2,1)S(1)} %collective-permute-done.20.refs_3_), channel_id=1, source_target_pairs={{0,4},{4,8},{8,12},{12,14},{14,10},{10,6},{6,2},{2,0},{1,5},{5,9},... | collective-permute-start | bytes 700424 | tf_op jit(solution)/shard_map/ppermute | solution.py:126
  32.9 9.0 %collective-permute-start.23 = (bf16[16,7296]{1,0:T(8,128)(2,1)S(1)}, bf16[16,7296]{1,0:T(8,128)(2,1)S(1)}, u32[]{:S(2)}, u32[]{:S(2)}) collective-permute-start(bf16[16,7296]{1,0:T(8,128)(2,1)S(1)} %collective-permute-done.21.refs_4_), channel_id=1, source_target_pairs={{0,2},{4,0},{8,4},{12,8},{14,12},{10,14},{6,10},{2,6},{1,3},{5,1},... | collective-permute-start | bytes 700424 | tf_op jit(solution)/shard_map/ppermute | solution.py:129
  39.8 9.6 %collective-permute-start.6 = (bf16[8,7296]{1,0:T(8,128)(2,1)S(1)}, bf16[8,7296]{1,0:T(8,128)(2,1)S(1)}, u32[]{:S(2)}, u32[]{:S(2)}) collective-permute-start(bf16[8,7296]{1,0:T(8,128)(2,1)S(1)} %slice.33), channel_id=1, source_target_pairs={{0,4},{4,8},{8,12},{12,14},{14,10},{10,6},{6,2},{2,0},{1,5},{5,9},... | collective-permute-start | bytes 350216 | tf_op jit(solution)/shard_map/ppermute | solution.py:126
  40.3 9.1 %collective-permute-start.7 = (bf16[8,7296]{1,0:T(8,128)(2,1)S(1)}, bf16[8,7296]{1,0:T(8,128)(2,1)S(1)}, u32[]{:S(2)}, u32[]{:S(2)}) collective-permute-start(bf16[8,7296]{1,0:T(8,128)(2,1)S(1)} %slice.34), channel_id=1, source_target_pairs={{0,2},{4,0},{8,4},{12,8},{14,12},{10,14},{6,10},{2,6},{1,3},{5,1},... | collective-permute-start | bytes 350216 | tf_op jit(solution)/shard_map/ppermute | solution.py:129
  42.0 12.8 %collective-permute-start.24 = (bf16[8,7296]{1,0:T(8,128)(2,1)S(1)}, bf16[8,7296]{1,0:T(8,128)(2,1)S(1)}, u32[]{:S(2)}, u32[]{:S(2)}) collective-permute-start(bf16[8,7296]{1,0:T(8,128)(2,1)S(1)} %slice.36), channel_id=1, source_target_pairs={{0,4},{4,8},{8,12},{12,14},{14,10},{10,6},{6,2},{2,0},{1,5},{5,9},... | collective-permute-start | bytes 350216 | tf_op jit(solution)/shard_map/ppermute | solution.py:126
  42.5 12.3 %collective-permute-start.25 = (bf16[8,7296]{1,0:T(8,128)(2,1)S(1)}, bf16[8,7296]{1,0:T(8,128)(2,1)S(1)}, u32[]{:S(2)}, u32[]{:S(2)}) collective-permute-start(bf16[8,7296]{1,0:T(8,128)(2,1)S(1)} %slice.37), channel_id=1, source_target_pairs={{0,2},{4,0},{8,4},{12,8},{14,12},{10,14},{6,10},{2,6},{1,3},{5,1},... | collective-permute-start | bytes 350216 | tf_op jit(solution)/shard_map/ppermute | solution.py:129
  52.7 7.5 %collective-permute-start.10 = (bf16[8,7168]{1,0:T(8,128)(2,1)S(1)}, bf16[8,7168]{1,0:T(8,128)(2,1)S(1)}, u32[]{:S(2)}, u32[]{:S(2)}) collective-permute-start(bf16[8,7168]{1,0:T(8,128)(2,1)S(1)} %get-tuple-element.24), channel_id=1, source_target_pairs={{0,4},{4,8},{8,12},{12,14},{14,10},{10,6},{6,2},{2,0},{1,5},{5,9},... | collective-permute-start | bytes 344072 | tf_op jit(solution)/shard_map/ppermute | solution.py:126
  53.2 7.5 %collective-permute-start.14 = (bf16[8,7168]{1,0:T(8,128)(2,1)S(1)}, bf16[8,7168]{1,0:T(8,128)(2,1)S(1)}, u32[]{:S(2)}, u32[]{:S(2)}) collective-permute-start(bf16[8,7168]{1,0:T(8,128)(2,1)S(1)} %get-tuple-element.28), channel_id=1, source_target_pairs={{0,2},{4,0},{8,4},{12,8},{14,12},{10,14},{6,10},{2,6},{1,3},{5,1},... | collective-permute-start | bytes 344072 | tf_op jit(solution)/shard_map/ppermute | solution.py:129
  58.1 6.1 %collective-permute-start.26 = (bf16[8,7168]{1,0:T(8,128)(2,1)S(1)}, bf16[8,7168]{1,0:T(8,128)(2,1)S(1)}, u32[]{:S(2)}, u32[]{:S(2)}) collective-permute-start(bf16[8,7168]{1,0:T(8,128)(2,1)S(1)} %get-tuple-element.33), channel_id=1, source_target_pairs={{0,4},{4,8},{8,12},{12,14},{14,10},{10,6},{6,2},{2,0},{1,5},{5,9},... | collective-permute-start | bytes 344072 | tf_op jit(solution)/shard_map/ppermute | solution.py:126
  58.6 6.1 %collective-permute-start.30 = (bf16[8,7168]{1,0:T(8,128)(2,1)S(1)}, bf16[8,7168]{1,0:T(8,128)(2,1)S(1)}, u32[]{:S(2)}, u32[]{:S(2)}) collective-permute-start(bf16[8,7168]{1,0:T(8,128)(2,1)S(1)} %get-tuple-element.37), channel_id=1, source_target_pairs={{0,2},{4,0},{8,4},{12,8},{14,12},{10,14},{6,10},{2,6},{1,3},{5,1},... | collective-permute-start | bytes 344072 | tf_op jit(solution)/shard_map/ppermute | solution.py:129
  60.2 8.9 %collective-permute-start.11 = (bf16[16,7168]{1,0:T(8,128)(2,1)S(1)}, bf16[16,7168]{1,0:T(8,128)(2,1)S(1)}, u32[]{:S(2)}, u32[]{:S(2)}) collective-permute-start(bf16[16,7168]{1,0:T(8,128)(2,1)S(1)} %add_convert_fusion.13), channel_id=1, source_target_pairs={{0,4},{4,8},{8,12},{12,14},{14,10},{10,6},{6,2},{2,0},{1,5},{5,9},... | collective-permute-start | bytes 688136 | tf_op jit(solution)/shard_map/ppermute | solution.py:126
  60.7 8.9 %collective-permute-start.15 = (bf16[16,7168]{1,0:T(8,128)(2,1)S(1)}, bf16[16,7168]{1,0:T(8,128)(2,1)S(1)}, u32[]{:S(2)}, u32[]{:S(2)}) collective-permute-start(bf16[16,7168]{1,0:T(8,128)(2,1)S(1)} %add_convert_fusion.10), channel_id=1, source_target_pairs={{0,2},{4,0},{8,4},{12,8},{14,12},{10,14},{6,10},{2,6},{1,3},{5,1},... | collective-permute-start | bytes 688136 | tf_op jit(solution)/shard_map/ppermute | solution.py:129
  64.2 9.8 %collective-permute-start.27 = (bf16[16,7168]{1,0:T(8,128)(2,1)S(1)}, bf16[16,7168]{1,0:T(8,128)(2,1)S(1)}, u32[]{:S(2)}, u32[]{:S(2)}) collective-permute-start(bf16[16,7168]{1,0:T(8,128)(2,1)S(1)} %add_convert_fusion.6), channel_id=1, source_target_pairs={{0,4},{4,8},{8,12},{12,14},{14,10},{10,6},{6,2},{2,0},{1,5},{5,9},... | collective-permute-start | bytes 688136 | tf_op jit(solution)/shard_map/ppermute | solution.py:126
  64.7 9.8 %collective-permute-start.31 = (bf16[16,7168]{1,0:T(8,128)(2,1)S(1)}, bf16[16,7168]{1,0:T(8,128)(2,1)S(1)}, u32[]{:S(2)}, u32[]{:S(2)}) collective-permute-start(bf16[16,7168]{1,0:T(8,128)(2,1)S(1)} %add_convert_fusion.3), channel_id=1, source_target_pairs={{0,2},{4,0},{8,4},{12,8},{14,12},{10,14},{6,10},{2,6},{1,3},{5,1},... | collective-permute-start | bytes 688136 | tf_op jit(solution)/shard_map/ppermute | solution.py:129
  69.1 9.8 %collective-permute-start.12 = (bf16[16,7168]{1,0:T(8,128)(2,1)S(1)}, bf16[16,7168]{1,0:T(8,128)(2,1)S(1)}, u32[]{:S(2)}, u32[]{:S(2)}) collective-permute-start(bf16[16,7168]{1,0:T(8,128)(2,1)S(1)} %add_convert_fusion.12), channel_id=1, source_target_pairs={{0,4},{4,8},{8,12},{12,14},{14,10},{10,6},{6,2},{2,0},{1,5},{5,9},... | collective-permute-start | bytes 688136 | tf_op jit(solution)/shard_map/ppermute | solution.py:126
  69.6 9.8 %collective-permute-start.16 = (bf16[16,7168]{1,0:T(8,128)(2,1)S(1)}, bf16[16,7168]{1,0:T(8,128)(2,1)S(1)}, u32[]{:S(2)}, u32[]{:S(2)}) collective-permute-start(bf16[16,7168]{1,0:T(8,128)(2,1)S(1)} %add_convert_fusion.9), channel_id=1, source_target_pairs={{0,2},{4,0},{8,4},{12,8},{14,12},{10,14},{6,10},{2,6},{1,3},{5,1},... | collective-permute-start | bytes 688136 | tf_op jit(solution)/shard_map/ppermute | solution.py:129
  74.0 9.8 %collective-permute-start.28 = (bf16[16,7168]{1,0:T(8,128)(2,1)S(1)}, bf16[16,7168]{1,0:T(8,128)(2,1)S(1)}, u32[]{:S(2)}, u32[]{:S(2)}) collective-permute-start(bf16[16,7168]{1,0:T(8,128)(2,1)S(1)} %add_convert_fusion.5), channel_id=1, source_target_pairs={{0,4},{4,8},{8,12},{12,14},{14,10},{10,6},{6,2},{2,0},{1,5},{5,9},... | collective-permute-start | bytes 688136 | tf_op jit(solution)/shard_map/ppermute | solution.py:126
  74.5 9.8 %collective-permute-start.32 = (bf16[16,7168]{1,0:T(8,128)(2,1)S(1)}, bf16[16,7168]{1,0:T(8,128)(2,1)S(1)}, u32[]{:S(2)}, u32[]{:S(2)}) collective-permute-start(bf16[16,7168]{1,0:T(8,128)(2,1)S(1)} %add_convert_fusion.2), channel_id=1, source_target_pairs={{0,2},{4,0},{8,4},{12,8},{14,12},{10,14},{6,10},{2,6},{1,3},{5,1},... | collective-permute-start | bytes 688136 | tf_op jit(solution)/shard_map/ppermute | solution.py:129
  78.9 8.4 %collective-permute-start.13 = (bf16[16,7168]{1,0:T(8,128)(2,1)S(1)}, bf16[16,7168]{1,0:T(8,128)(2,1)S(1)}, u32[]{:S(2)}, u32[]{:S(2)}) collective-permute-start(bf16[16,7168]{1,0:T(8,128)(2,1)S(1)} %add_convert_fusion.11), channel_id=1, source_target_pairs={{0,4},{4,8},{8,12},{12,14},{14,10},{10,6},{6,2},{2,0},{1,5},{5,9},... | collective-permute-start | bytes 688136 | tf_op jit(solution)/shard_map/ppermute | solution.py:126
  79.5 8.3 %collective-permute-start.17 = (bf16[16,7168]{1,0:T(8,128)(2,1)S(1)}, bf16[16,7168]{1,0:T(8,128)(2,1)S(1)}, u32[]{:S(2)}, u32[]{:S(2)}) collective-permute-start(bf16[16,7168]{1,0:T(8,128)(2,1)S(1)} %add_convert_fusion.8), channel_id=1, source_target_pairs={{0,2},{4,0},{8,4},{12,8},{14,12},{10,14},{6,10},{2,6},{1,3},{5,1},... | collective-permute-start | bytes 688136 | tf_op jit(solution)/shard_map/ppermute | solution.py:129
  83.8 6.1 %collective-permute-start.29 = (bf16[16,7168]{1,0:T(8,128)(2,1)S(1)}, bf16[16,7168]{1,0:T(8,128)(2,1)S(1)}, u32[]{:S(2)}, u32[]{:S(2)}) collective-permute-start(bf16[16,7168]{1,0:T(8,128)(2,1)S(1)} %add_convert_fusion.4), channel_id=1, source_target_pairs={{0,4},{4,8},{8,12},{12,14},{14,10},{10,6},{6,2},{2,0},{1,5},{5,9},... | collective-permute-start | bytes 688136 | tf_op jit(solution)/shard_map/ppermute | solution.py:126
  84.4 6.1 %collective-permute-start.33 = (bf16[16,7168]{1,0:T(8,128)(2,1)S(1)}, bf16[16,7168]{1,0:T(8,128)(2,1)S(1)}, u32[]{:S(2)}, u32[]{:S(2)}) collective-permute-start(bf16[16,7168]{1,0:T(8,128)(2,1)S(1)} %add_convert_fusion.1), channel_id=1, source_target_pairs={{0,2},{4,0},{8,4},{12,8},{14,12},{10,14},{6,10},{2,6},{1,3},{5,1},... | collective-permute-start | bytes 688136 | tf_op jit(solution)/shard_map/ppermute | solution.py:129
where the time goes:
time: 91.5 us; the launch traced here: 91.3 us
  starting transfers between devices  40 us (44%)
  waiting for transfers between devices  30.6 us (33%)
  Pallas kernels  17 us (19%)
  other arithmetic  2.27 us (2%)
  local copies, waits for them, and re-layouts  1.27 us (1%)
    ppermute x16, waiting for transfers between devices, on(): return lax.ppermute(x, 'ep', onward)  29.6 us
    ppermute x16, starting transfers between devices, back(): return lax.ppermute(x, 'ep', backward)  25 us
    ppermute x16, starting transfers between devices, on(): return lax.ppermute(x, 'ep', onward)  14.4 us
    pallas_call x4, Pallas kernels, resident(): pl.pallas_call(body, out_shape=pltpu.VMEM(x.shape, x.dtype), in_specs=[pl...  10.4 us
    pallas_call x2, Pallas kernels, apply_experts(): pl.pallas_call(functools.partial(expert_body, width, inner, node_size, le...  6.58 us
  transfers between devices with their start and end apart: 34, of which 14 were waited for; matrix products, arithmetic and copies ran while one was open for 3% of the time, Pallas kernels for 19%

commit v1 on v0

--- a/solution.py
+++ b/solution.py
@@ -58,13 +58,72 @@
     )(pltpu.with_memory_space_constraint(x, pltpu.HBM))
 
 
-def expert_body(width, inner, node_size, local_count, block_count, *refs):
+def pack_body(expert_total, ids_ref, gates_ref, tokens_ref, *refs):
+    out_refs, (ids_held, gates_held, sems) = refs[:SUBSETS], refs[SUBSETS:]
+    rows = out_refs[0].shape[0]
+    width = tokens_ref.shape[1]
+    first = [
+        pltpu.make_async_copy(ids_ref, ids_held, sems.at[SUBSETS]),
+        pltpu.make_async_copy(gates_ref, gates_held, sems.at[SUBSETS + 1]),
+    ]
+    then = [
+        pltpu.make_async_copy(tokens_ref.at[pl.ds(s * rows, rows)], out.at[:, pl.ds(0, width)], sems.at[s])
+        for s, out in enumerate(out_refs)
+    ]
+    for copy in first + then:
+        copy.start()
+    for copy in first:
+        copy.wait()
+    ids, gates = ids_held[...], gates_held[...]
+    rest = jnp.concatenate(
+        [jnp.sum(jnp.where(ids == e, gates, 0.0), axis=0, keepdims=True) for e in range(expert_total)], axis=0
+    )
+    parts = []
+    for _ in range(3):
+        part = rest.astype(jnp.bfloat16).astype(jnp.float32)
+        rest = rest - part
+        parts.append(part)
+    side = jnp.concatenate(parts, axis=0).T
+    side = jnp.concatenate([side[s * rows : (s + 1) * rows] for s in range(SUBSETS)], axis=1)
+    empty = out_refs[0].shape[1] - width - side.shape[1]
+    if empty:
+        side = jnp.concatenate([side, jnp.zeros((rows, empty), jnp.float32)], axis=1)
+    out_refs[0][:, width:] = side.astype(jnp.bfloat16)
+    for copy in then:
+        copy.wait()
+
+
+def pack(tokens, expert_ids, gate_weights, expert_total):
+    token_count, width = tokens.shape
+    rows = token_count // SUBSETS
+    inputs = [pltpu.with_memory_space_constraint(x, pltpu.HBM) for x in (expert_ids.T, gate_weights.T, tokens)]
+    return pl.pallas_call(
+        functools.partial(pack_body, expert_total),
+        out_shape=[
+            jax.ShapeDtypeStruct((rows, width + (0 if s else side_columns(expert_total))), tokens.dtype)
+            for s in range(SUBSETS)
+        ],
+        in_specs=[pl.BlockSpec(memory_space=pltpu.HBM)] * 3,
+        out_specs=[pl.BlockSpec(memory_space=pltpu.VMEM)] * SUBSETS,
+        scratch_shapes=[
+            pltpu.VMEM(inputs[0].shape, jnp.int32),
+            pltpu.VMEM(inputs[1].shape, jnp.float32),
+            pltpu.SemaphoreType.DMA((SUBSETS + 2,)),
+        ],
+        compiler_params=pltpu.CompilerParams(vmem_limit_bytes=4 << 20),
+    )(*inputs)
+
+
+def expert_body(subset, node_size, local_count, block_count, side_count, *refs):
     expert_count = node_size * local_count
     expert_total = lax.axis_size("ep") * expert_count
     blocks = refs[:block_count]
-    ups = refs[block_count : block_count + expert_count]
-    downs = refs[block_count + expert_count : block_count + 2 * expert_count]
-    out_refs, x_ref = refs[block_count + 2 * expert_count : -1], refs[-1]
+    sides = refs[block_count : block_count + side_count]
+    weights = refs[block_count + side_count :]
+    ups = weights[:expert_count]
+    downs = weights[expert_count : 2 * expert_count]
+    out_refs = weights[2 * expert_count :]
+    inner, width = downs[0].shape
     me = lax.axis_index("ep") * node_size
     core = lax.axis_index("node")
     numbers = [
@@ -72,24 +131,28 @@
         for shift in range(node_size)
         for local in range(local_count)
     ]
-    row = 0
-    for block in blocks:
-        x_ref[row : row + block.shape[0], :] = block[...]
-        row += block.shape[0]
-    side = x_ref[:, width:].astype(jnp.float32)
-    lane = lax.broadcasted_iota(jnp.int32, side.shape, 1)
-    hidden, scales = [], []
-    for e in range(expert_count):
-        total = jnp.dot(x_ref[:, :width], ups[e][...], preferred_element_type=jnp.float32)
-        hidden.append((jax.nn.silu(total[:, :inner]) * total[:, inner:]).astype(jnp.bfloat16))
+    side_width = side_columns(expert_total)
+    side = jnp.concatenate([ref[:, ref.shape[1] - side_width :] for ref in sides], axis=0).astype(jnp.float32)
+    lane = lax.broadcasted_iota(jnp.int32, side.shape, 1) - subset * 3 * expert_total
+    depth = 1024 if width % 1024 == 0 else width
+    totals = [None] * expert_count
+    for k in range(width // depth):
+        at = slice(k * depth, (k + 1) * depth)
+        x = jnp.concatenate([block[:, at] for block in blocks], axis=0)
+        for e in range(expert_count):
+            part = jnp.dot(x, ups[e][at, :], preferred_element_type=jnp.float32)
+            totals[e] = part if totals[e] is None else totals[e] + part
+    hidden = []
+    for e, total in enumerate(totals):
         mine = (lane == numbers[e]) | (lane == numbers[e] + expert_total) | (lane == numbers[e] + 2 * expert_total)
-        scales.append(jnp.sum(jnp.where(mine, side, 0.0), axis=1, keepdims=True))
+        scale = jnp.sum(jnp.where(mine, side, 0.0), axis=1, keepdims=True)
+        hidden.append((scale * (jax.nn.silu(total[:, :inner]) * total[:, inner:])).astype(jnp.bfloat16))
     tile = 512 if width % 512 == 0 else LANES
     for n in range(width // tile):
         at = slice(n * tile, (n + 1) * tile)
         y = None
         for e in range(expert_count):
-            part = scales[e] * jnp.dot(hidden[e], downs[e][:, at], preferred_element_type=jnp.float32)
+            part = jnp.dot(hidden[e], downs[e][:, at], preferred_element_type=jnp.float32)
             y = part if y is None else y + part
         row = 0
         for out in out_refs:
@@ -97,18 +160,21 @@
             row += out.shape[0]
 
 
-def apply_experts(blocks, dtypes, ups, downs, node_size):
+def side_columns(expert_total):
+    return -(-SUBSETS * 3 * expert_total // LANES) * LANES
+
+
+def apply_experts(subset, blocks, sides, dtypes, ups, downs, node_size):
     inner, width = downs[0].shape
     rows = sum(block.shape[0] for block in blocks)
     vmem = pl.BlockSpec(memory_space=pltpu.VMEM)
     weights = [pltpu.with_memory_space_constraint(x, pltpu.VMEM) for x in (*ups, *downs)]
-    inputs = [*blocks, *weights]
+    inputs = [*blocks, *sides, *weights]
     return pl.pallas_call(
-        functools.partial(expert_body, width, inner, node_size, len(ups) // node_size, len(blocks)),
+        functools.partial(expert_body, subset, node_size, len(ups) // node_size, len(blocks), len(sides)),
         out_shape=[jax.ShapeDtypeStruct((b.shape[0], width), dtype) for b, dtype in zip(blocks, dtypes)],
         in_specs=[vmem] * len(inputs),
         out_specs=[vmem] * len(blocks),
-        scratch_shapes=[pltpu.VMEM((rows, blocks[0].shape[1]), jnp.bfloat16)],
         compiler_params=pltpu.CompilerParams(vmem_limit_bytes=12 << 20),
         cost_estimate=pl.CostEstimate(
             flops=6 * rows * width * inner * len(ups), bytes_accessed=rows * width * 6, transcendentals=rows * inner
@@ -160,29 +226,22 @@
         token_count, _ = tokens.shape
         local_count = gate_up_weight.shape[0]
         expert_total = count * node_size * local_count
-        chosen = expert_ids[:, :, None] == jnp.arange(expert_total, dtype=jnp.int32)
-        rest = jnp.sum(jnp.where(chosen, gate_weights[:, :, None], 0.0), axis=1)
-        parts = []
-        for _ in range(3):
-            part = lax.reduce_precision(rest, 8, 7)
-            rest = rest - part
-            parts.append(part)
-        side = jnp.concatenate(parts, axis=1).astype(jnp.bfloat16)
-        side = jnp.pad(side, ((0, 0), (0, -side.shape[1] % LANES)))
+        rows = token_count // SUBSETS
+        subsets = pack(tokens, expert_ids, gate_weights, expert_total)
+        gathered = [gather(own) for own in subsets]
+        sides = gathered[0]
         ups, downs = [], []
         for shift in range(node_size):
             up, down = gate_up_weight, down_weight
             if shift:
                 ring = [(i, (i - shift) % node_size) for i in range(node_size)]
-                up, down = lax.ppermute((up, down), "node", ring)
+                up = lax.ppermute(up, "node", ring)
+                down = lax.ppermute(down, "node", ring)
             for local in range(local_count):
                 for held, weight in ((ups, up[local]), (downs, down[local])):
-                    held.append(resident(weight))
-        rows = token_count // SUBSETS
-        gathered = []
-        for s in range(SUBSETS):
-            at = slice(s * rows, (s + 1) * rows)
-            gathered.append(gather(jnp.concatenate([tokens[at], side[at]], axis=1)))
+                    if not shift:
+                        weight = resident(weight)
+                    held.append(weight)
         outs = []
         for s in range(SUBSETS):
             blocks, sums = gathered[s], []
@@ -191,7 +250,7 @@
             starts = list(range(len(blocks), 0, -per_call))
             for end in reversed(starts):
                 at = slice(max(0, end - per_call), end)
-                sums += apply_experts(blocks[at], dtypes[at], ups, downs, node_size)
+                sums += apply_experts(s, blocks[at], sides[at], dtypes[at], ups, downs, node_size)
             outs.append(scatter(sums))
         return jnp.concatenate(outs, axis=0)
 

time: 91.5 us -> 89.2 us (0.975)
  Pallas kernels: 17 us -> 12.7 us
  waiting for transfers between devices: 30.6 us -> 34.1 us
  local copies, waits for them, and re-layouts: 1.27 us -> 0.03 us
    ppermute x16, waiting for transfers between devices: 1 us -> 15.1 us  [back(): return lax.ppermute(x, 'ep', backward)]
    ppermute x16, waiting for transfers between devices: 29.6 us -> 19 us  [on(): return lax.ppermute(x, 'ep', onward)]
    pallas_call x4 -> x2, Pallas kernels: 10.4 us -> 5.23 us  [resident(): pl.pallas_call(body, out_shape=pltpu.VMEM(x.shape, x.dtype), in_specs=[pl...]
    ppermute x16, starting transfers between devices: 25 us -> 27 us  [back(): return lax.ppermute(x, 'ep', backward)]
    ppermute x16, starting transfers between devices: 14.4 us -> 13.1 us  [on(): return lax.ppermute(x, 'ep', onward)]
    slice x2 -> x0, local copies, waits for them, and re-layouts: 1.08 us -> none  [on_device(): gathered.append(gather(jnp.concatenate([tokens[at], side[at]], axis=1)))]
    pallas_call x2 -> x3, Pallas kernels: 6.58 us -> 7.47 us  [the longest x2 6.36 us: apply_experts(): pl.pallas_call(functools.partial(expert_body, subset, node_size, len(ups)...]
  transfers between devices with their start and end apart: 34 -> 34, of which waited for: 14 -> 17; matrix products, arithmetic and copies ran while one was open for 3% -> 1% of each run, Pallas kernels for 19% -> 11%
where the time goes in v1:
time: 89.2 us; the launch traced here: 89.1 us
  starting transfers between devices  40.6 us (46%)
  waiting for transfers between devices  34.1 us (38%)
  Pallas kernels  12.7 us (14%)
  other arithmetic  1.41 us (2%)
    ppermute x16, starting transfers between devices, back(): return lax.ppermute(x, 'ep', backward)  27 us
    ppermute x16, waiting for transfers between devices, on(): return lax.ppermute(x, 'ep', onward)  19 us
    ppermute x16, waiting for transfers between devices, back(): return lax.ppermute(x, 'ep', backward)  15.1 us
    ppermute x16, starting transfers between devices, on(): return lax.ppermute(x, 'ep', onward)  13.1 us
    pallas_call x2, Pallas kernels, apply_experts(): pl.pallas_call(functools.partial(expert_body, subset, node_size, len(ups)...  6.36 us
    pallas_call x2, Pallas kernels, resident(): pl.pallas_call(body, out_shape=pltpu.VMEM(x.shape, x.dtype), in_specs=[pl...  5.23 us
  transfers between devices with their start and end apart: 34, of which 17 were waited for; matrix products, arithmetic and copies ran while one was open for 1% of the time, Pallas kernels for 11%

profile of v1, /device:TPU:0, one launch (start us, length us, event | category | flops | bytes accessed | tf_op | source)
XLA Modules:
  0.0 89.1 jit_solution(5880492261304742740)
XLA Ops:
  0.0 0.5 collective-permute-start.8
  0.5 1.1 %shard_map.55 = (bf16[16,7296]{1,0:T(8,128)(2,1)S(1)}, bf16[16,7168]{1,0:T(8,128)(2,1)S(1)}) custom-call(s32[8,32]{1,0:T(8,128)} %bitcast.12, f32[8,32]{1,0:T(8,128)} %bitcast.13, bf16[32,7168]{1,0:T(8,128)(2,1)} %tokens_ref.1), custom_call_target="tpu_custom_call" | custom-call | tf_op jit(solution)/shard_map/pallas_call | solution.py:100
  1.6 3.1 %collective-permute-start.18 = (bf16[16,7168]{1,0:T(8,128)(2,1)S(1)}, bf16[16,7168]{1,0:T(8,128)(2,1)S(1)}, u32[]{:S(2)}, u32[]{:S(2)}) collective-permute-start(bf16[16,7168]{1,0:T(8,128)(2,1)S(1)} %get-tuple-element.35.refs_0_), channel_id=1, source_target_pairs={{0,4},{4,8},{8,12},{12,14},{14,10},{10,6},{6,2},{2,0},{1,5},{5,9},... | collective-permute-start | bytes 688136 | tf_op jit(solution)/shard_map/ppermute | solution.py:192
  4.7 2.0 %collective-permute-start = (bf16[16,7296]{1,0:T(8,128)(2,1)S(1)}, bf16[16,7296]{1,0:T(8,128)(2,1)S(1)}, u32[]{:S(2)}, u32[]{:S(2)}) collective-permute-start(bf16[16,7296]{1,0:T(8,128)(2,1)S(1)} %get-tuple-element.25.refs_0_.refs_9_), channel_id=1, source_target_pairs={{0,4},{4,8},{8,12},{12,14},{14,10},{10,6},{6,2},{2,0},{1,5},{5,9},... | collective-permute-start | bytes 700424 | tf_op jit(solution)/shard_map/ppermute | solution.py:192
  6.8 4.4 %collective-permute-done.18.refs_1_ = bf16[16,7168]{1,0:T(8,128)(2,1)S(1)} collective-permute-done((bf16[16,7168]{1,0:T(8,128)(2,1)S(1)}, bf16[16,7168]{1,0:T(8,128)(2,1)S(1)}, u32[]{:S(2)}, u32[]{:S(2)}) %collective-permute-start.18) | collective-permute-done | bytes 229408 | tf_op jit(solution)/shard_map/ppermute | solution.py:192
  11.1 2.0 %collective-permute-start.1 = (bf16[16,7296]{1,0:T(8,128)(2,1)S(1)}, bf16[16,7296]{1,0:T(8,128)(2,1)S(1)}, u32[]{:S(2)}, u32[]{:S(2)}) collective-permute-start(bf16[16,7296]{1,0:T(8,128)(2,1)S(1)} %get-tuple-element.25.refs_0_.refs_9_), channel_id=1, source_target_pairs={{0,2},{4,0},{8,4},{12,8},{14,12},{10,14},{6,10},{2,6},{1,3},{5,1},... | collective-permute-start | bytes 700424 | tf_op jit(solution)/shard_map/ppermute | solution.py:195
  13.2 0.4 collective-permute-start.20
  13.5 2.6 %collective-permute-done.refs_1_.refs_10_ = bf16[16,7296]{1,0:T(8,128)(2,1)S(1)} collective-permute-done((bf16[16,7296]{1,0:T(8,128)(2,1)S(1)}, bf16[16,7296]{1,0:T(8,128)(2,1)S(1)}, u32[]{:S(2)}, u32[]{:S(2)}) %collective-permute-start) | collective-permute-done | bytes 233504 | tf_op jit(solution)/shard_map/ppermute | solution.py:192
  16.1 2.0 %collective-permute-start.21 = (bf16[16,7168]{1,0:T(8,128)(2,1)S(1)}, bf16[16,7168]{1,0:T(8,128)(2,1)S(1)}, u32[]{:S(2)}, u32[]{:S(2)}) collective-permute-start(bf16[16,7168]{1,0:T(8,128)(2,1)S(1)} %collective-permute-done.19.refs_2_), channel_id=1, source_target_pairs={{0,2},{4,0},{8,4},{12,8},{14,12},{10,14},{6,10},{2,6},{1,3},{5,1},... | collective-permute-start | bytes 688136 | tf_op jit(solution)/shard_map/ppermute | solution.py:195
  18.2 1.4 %collective-permute-start.2 = (bf16[16,7296]{1,0:T(8,128)(2,1)S(1)}, bf16[16,7296]{1,0:T(8,128)(2,1)S(1)}, u32[]{:S(2)}, u32[]{:S(2)}) collective-permute-start(bf16[16,7296]{1,0:T(8,128)(2,1)S(1)} %collective-permute-done.refs_1_.refs_10_), channel_id=1, source_target_pairs={{0,4},{4,8},{8,12},{12,14},{14,10},{10,6},{6,2},{2,0},{1,5},{5,9},... | collective-permute-start | bytes 700424 | tf_op jit(solution)/shard_map/ppermute | solution.py:192
  19.6 2.1 %collective-permute-done.20.refs_3_ = bf16[16,7168]{1,0:T(8,128)(2,1)S(1)} collective-permute-done((bf16[16,7168]{1,0:T(8,128)(2,1)S(1)}, bf16[16,7168]{1,0:T(8,128)(2,1)S(1)}, u32[]{:S(2)}, u32[]{:S(2)}) %collective-permute-start.20) | collective-permute-done | bytes 229408 | tf_op jit(solution)/shard_map/ppermute | solution.py:192
  21.6 1.6 %collective-permute-start.3 = (bf16[16,7296]{1,0:T(8,128)(2,1)S(1)}, bf16[16,7296]{1,0:T(8,128)(2,1)S(1)}, u32[]{:S(2)}, u32[]{:S(2)}) collective-permute-start(bf16[16,7296]{1,0:T(8,128)(2,1)S(1)} %collective-permute-done.1.refs_2_.refs_11_), channel_id=1, source_target_pairs={{0,2},{4,0},{8,4},{12,8},{14,12},{10,14},{6,10},{2,6},{1,3},{5,1},... | collective-permute-start | bytes 700424 | tf_op jit(solution)/shard_map/ppermute | solution.py:195
  23.2 1.4 %collective-permute-start.22 = (bf16[16,7168]{1,0:T(8,128)(2,1)S(1)}, bf16[16,7168]{1,0:T(8,128)(2,1)S(1)}, u32[]{:S(2)}, u32[]{:S(2)}) collective-permute-start(bf16[16,7168]{1,0:T(8,128)(2,1)S(1)} %collective-permute-done.20.refs_3_), channel_id=1, source_target_pairs={{0,4},{4,8},{8,12},{12,14},{14,10},{10,6},{6,2},{2,0},{1,5},{5,9},... | collective-permute-start | bytes 688136 | tf_op jit(solution)/shard_map/ppermute | solution.py:192
  24.6 2.2 %collective-permute-done.2.refs_3_.refs_12_ = bf16[16,7296]{1,0:T(8,128)(2,1)S(1)} collective-permute-done((bf16[16,7296]{1,0:T(8,128)(2,1)S(1)}, bf16[16,7296]{1,0:T(8,128)(2,1)S(1)}, u32[]{:S(2)}, u32[]{:S(2)}) %collective-permute-start.2) | collective-permute-done | bytes 233504 | tf_op jit(solution)/shard_map/ppermute | solution.py:192
  26.7 1.6 %collective-permute-start.23 = (bf16[16,7168]{1,0:T(8,128)(2,1)S(1)}, bf16[16,7168]{1,0:T(8,128)(2,1)S(1)}, u32[]{:S(2)}, u32[]{:S(2)}) collective-permute-start(bf16[16,7168]{1,0:T(8,128)(2,1)S(1)} %collective-permute-done.21.refs_4_), channel_id=1, source_target_pairs={{0,2},{4,0},{8,4},{12,8},{14,12},{10,14},{6,10},{2,6},{1,3},{5,1},... | collective-permute-start | bytes 688136 | tf_op jit(solution)/shard_map/ppermute | solution.py:195
  28.3 1.3 %collective-permute-start.4 = (bf16[16,7296]{1,0:T(8,128)(2,1)S(1)}, bf16[16,7296]{1,0:T(8,128)(2,1)S(1)}, u32[]{:S(2)}, u32[]{:S(2)}) collective-permute-start(bf16[16,7296]{1,0:T(8,128)(2,1)S(1)} %collective-permute-done.2.refs_3_.refs_12_), channel_id=1, source_target_pairs={{0,4},{4,8},{8,12},{12,14},{14,10},{10,6},{6,2},{2,0},{1,5},{5,9},... | collective-permute-start | bytes 700424 | tf_op jit(solution)/shard_map/ppermute | solution.py:192
  29.6 2.1 %collective-permute-done.22.refs_5_ = bf16[16,7168]{1,0:T(8,128)(2,1)S(1)} collective-permute-done((bf16[16,7168]{1,0:T(8,128)(2,1)S(1)}, bf16[16,7168]{1,0:T(8,128)(2,1)S(1)}, u32[]{:S(2)}, u32[]{:S(2)}) %collective-permute-start.22) | collective-permute-done | bytes 229408 | tf_op jit(solution)/shard_map/ppermute | solution.py:192
  31.7 1.6 %collective-permute-start.5 = (bf16[16,7296]{1,0:T(8,128)(2,1)S(1)}, bf16[16,7296]{1,0:T(8,128)(2,1)S(1)}, u32[]{:S(2)}, u32[]{:S(2)}) collective-permute-start(bf16[16,7296]{1,0:T(8,128)(2,1)S(1)} %collective-permute-done.3.refs_4_.refs_13_), channel_id=1, source_target_pairs={{0,2},{4,0},{8,4},{12,8},{14,12},{10,14},{6,10},{2,6},{1,3},{5,1},... | collective-permute-start | bytes 700424 | tf_op jit(solution)/shard_map/ppermute | solution.py:195
  33.4 1.1 %collective-permute-start.24 = (bf16[8,7168]{1,0:T(8,128)(2,1)S(1)}, bf16[8,7168]{1,0:T(8,128)(2,1)S(1)}, u32[]{:S(2)}, u32[]{:S(2)}) collective-permute-start(bf16[8,7168]{1,0:T(8,128)(2,1)S(1)} %slice.18), channel_id=1, source_target_pairs={{0,4},{4,8},{8,12},{12,14},{14,10},{10,6},{6,2},{2,0},{1,5},{5,9},... | collective-permute-start | bytes 344072 | tf_op jit(solution)/shard_map/ppermute | solution.py:192
  34.5 2.0 %collective-permute-done.4.refs_5_.refs_14_ = bf16[16,7296]{1,0:T(8,128)(2,1)S(1)} collective-permute-done((bf16[16,7296]{1,0:T(8,128)(2,1)S(1)}, bf16[16,7296]{1,0:T(8,128)(2,1)S(1)}, u32[]{:S(2)}, u32[]{:S(2)}) %collective-permute-start.4) | collective-permute-done | bytes 233504 | tf_op jit(solution)/shard_map/ppermute | solution.py:192
  36.5 1.7 %collective-permute-start.25 = (bf16[8,7168]{1,0:T(8,128)(2,1)S(1)}, bf16[8,7168]{1,0:T(8,128)(2,1)S(1)}, u32[]{:S(2)}, u32[]{:S(2)}) collective-permute-start(bf16[8,7168]{1,0:T(8,128)(2,1)S(1)} %slice.19), channel_id=1, source_target_pairs={{0,2},{4,0},{8,4},{12,8},{14,12},{10,14},{6,10},{2,6},{1,3},{5,1},... | collective-permute-start | bytes 344072 | tf_op jit(solution)/shard_map/ppermute | solution.py:195
  38.3 0.2 collective-permute-done.5.refs_6_.refs_15_
  38.5 1.1 %collective-permute-start.6 = (bf16[8,7296]{1,0:T(8,128)(2,1)S(1)}, bf16[8,7296]{1,0:T(8,128)(2,1)S(1)}, u32[]{:S(2)}, u32[]{:S(2)}) collective-permute-start(bf16[8,7296]{1,0:T(8,128)(2,1)S(1)} %slice.16), channel_id=1, source_target_pairs={{0,4},{4,8},{8,12},{12,14},{14,10},{10,6},{6,2},{2,0},{1,5},{5,9},... | collective-permute-start | bytes 350216 | tf_op jit(solution)/shard_map/ppermute | solution.py:192
  39.6 1.0 %collective-permute-start.7 = (bf16[8,7296]{1,0:T(8,128)(2,1)S(1)}, bf16[8,7296]{1,0:T(8,128)(2,1)S(1)}, u32[]{:S(2)}, u32[]{:S(2)}) collective-permute-start(bf16[8,7296]{1,0:T(8,128)(2,1)S(1)} %slice.17), channel_id=1, source_target_pairs={{0,2},{4,0},{8,4},{12,8},{14,12},{10,14},{6,10},{2,6},{1,3},{5,1},... | collective-permute-start | bytes 350216 | tf_op jit(solution)/shard_map/ppermute | solution.py:195
  40.6 3.2 %shard_map.56.refs_18_ = bf16[7168,512]{1,0:T(8,128)(2,1)S(1)} custom-call(bf16[7168,512]{1,0:T(8,128)(2,1)} %bitcast.10), custom_call_target="tpu_custom_call" | custom-call | flops 1835008000 | bytes 14680064 | tf_op jit(solution)/shard_map/pallas_call | solution.py:50
  43.8 2.1 %shard_map.57.refs_20_ = bf16[256,7168]{1,0:T(8,128)(2,1)S(1)} custom-call(bf16[256,7168]{1,0:T(8,128)(2,1)} %bitcast.11), custom_call_target="tpu_custom_call" | custom-call | flops 917504000 | bytes 7340032 | tf_op jit(solution)/shard_map/pallas_call | solution.py:50
  45.9 3.2 %shard_map.59 = (f32[16,7168]{1,0:T(8,128)S(1)}, f32[16,7168]{1,0:T(8,128)S(1)}, f32[16,7168]{1,0:T(8,128)S(1)}, f32[16,7168]{1,0:T(8,128)S(1)}, f32[16,7168]{1,...) custom-call(bf16[16,7168]{1,0:T(8,128)(2,1)S(1)} %get-tuple-element., ...), custom_call_target="tpu_custom_call" | custom-call | flops 2818572288 | bytes 5505024 | tf_op jit(solution)/shard_map/pallas_call | solution.py:173
  49.1 1.9 %collective-permute-start.30 = (bf16[8,7168]{1,0:T(8,128)(2,1)S(1)}, bf16[8,7168]{1,0:T(8,128)(2,1)S(1)}, u32[]{:S(2)}, u32[]{:S(2)}) collective-permute-start(bf16[8,7168]{1,0:T(8,128)(2,1)S(1)} %get-tuple-element.41), channel_id=1, source_target_pairs={{0,2},{4,0},{8,4},{12,8},{14,12},{10,14},{6,10},{2,6},{1,3},{5,1},... | collective-permute-start | bytes 344072 | tf_op jit(solution)/shard_map/ppermute | solution.py:195
  51.2 3.2 %shard_map.58 = (f32[16,7168]{1,0:T(8,128)S(1)}, f32[16,7168]{1,0:T(8,128)S(1)}, f32[16,7168]{1,0:T(8,128)S(1)}, f32[16,7168]{1,0:T(8,128)S(1)}, f32[16,7168]{1,...) custom-call(bf16[16,7296]{1,0:T(8,128)(2,1)S(1)} %get-tuple-element., ...), custom_call_target="tpu_custom_call" | custom-call | flops 2818572288 | bytes 5505024 | tf_op jit(solution)/shard_map/pallas_call | solution.py:173
  54.4 1.9 %collective-permute-start.14 = (bf16[8,7168]{1,0:T(8,128)(2,1)S(1)}, bf16[8,7168]{1,0:T(8,128)(2,1)S(1)}, u32[]{:S(2)}, u32[]{:S(2)}) collective-permute-start(bf16[8,7168]{1,0:T(8,128)(2,1)S(1)} %get-tuple-element.31), channel_id=1, source_target_pairs={{0,2},{4,0},{8,4},{12,8},{14,12},{10,14},{6,10},{2,6},{1,3},{5,1},... | collective-permute-start | bytes 344072 | tf_op jit(solution)/shard_map/ppermute | solution.py:195
  56.5 1.9 %collective-permute-start.31 = (bf16[16,7168]{1,0:T(8,128)(2,1)S(1)}, bf16[16,7168]{1,0:T(8,128)(2,1)S(1)}, u32[]{:S(2)}, u32[]{:S(2)}) collective-permute-start(bf16[16,7168]{1,0:T(8,128)(2,1)S(1)} %add_convert_fusion.3), channel_id=1, source_target_pairs={{0,2},{4,0},{8,4},{12,8},{14,12},{10,14},{6,10},{2,6},{1,3},{5,1},... | collective-permute-start | bytes 688136 | tf_op jit(solution)/shard_map/ppermute | solution.py:195
  58.5 0.2 collective-permute-start.27
  58.7 1.8 %collective-permute-done.14 = bf16[8,7168]{1,0:T(8,128)(2,1)S(1)} collective-permute-done((bf16[8,7168]{1,0:T(8,128)(2,1)S(1)}, bf16[8,7168]{1,0:T(8,128)(2,1)S(1)}, u32[]{:S(2)}, u32[]{:S(2)}) %collective-permute-start.14) | collective-permute-done | bytes 114720 | tf_op jit(solution)/shard_map/ppermute | solution.py:195
  60.5 1.9 %collective-permute-start.15 = (bf16[16,7168]{1,0:T(8,128)(2,1)S(1)}, bf16[16,7168]{1,0:T(8,128)(2,1)S(1)}, u32[]{:S(2)}, u32[]{:S(2)}) collective-permute-start(bf16[16,7168]{1,0:T(8,128)(2,1)S(1)} %add_convert_fusion.10), channel_id=1, source_target_pairs={{0,2},{4,0},{8,4},{12,8},{14,12},{10,14},{6,10},{2,6},{1,3},{5,1},... | collective-permute-start | bytes 688136 | tf_op jit(solution)/shard_map/ppermute | solution.py:195
  62.6 2.7 %collective-permute-done.31 = bf16[16,7168]{1,0:T(8,128)(2,1)S(1)} collective-permute-done((bf16[16,7168]{1,0:T(8,128)(2,1)S(1)}, bf16[16,7168]{1,0:T(8,128)(2,1)S(1)}, u32[]{:S(2)}, u32[]{:S(2)}) %collective-permute-start.31) | collective-permute-done | bytes 229408 | tf_op jit(solution)/shard_map/ppermute | solution.py:195
  65.4 1.9 %collective-permute-start.32 = (bf16[16,7168]{1,0:T(8,128)(2,1)S(1)}, bf16[16,7168]{1,0:T(8,128)(2,1)S(1)}, u32[]{:S(2)}, u32[]{:S(2)}) collective-permute-start(bf16[16,7168]{1,0:T(8,128)(2,1)S(1)} %add_convert_fusion.2), channel_id=1, source_target_pairs={{0,2},{4,0},{8,4},{12,8},{14,12},{10,14},{6,10},{2,6},{1,3},{5,1},... | collective-permute-start | bytes 688136 | tf_op jit(solution)/shard_map/ppermute | solution.py:195
  67.4 0.2 collective-permute-start.28
  67.6 2.7 %collective-permute-done.15 = bf16[16,7168]{1,0:T(8,128)(2,1)S(1)} collective-permute-done((bf16[16,7168]{1,0:T(8,128)(2,1)S(1)}, bf16[16,7168]{1,0:T(8,128)(2,1)S(1)}, u32[]{:S(2)}, u32[]{:S(2)}) %collective-permute-start.15) | collective-permute-done | bytes 229408 | tf_op jit(solution)/shard_map/ppermute | solution.py:195
  70.3 1.9 %collective-permute-start.16 = (bf16[16,7168]{1,0:T(8,128)(2,1)S(1)}, bf16[16,7168]{1,0:T(8,128)(2,1)S(1)}, u32[]{:S(2)}, u32[]{:S(2)}) collective-permute-start(bf16[16,7168]{1,0:T(8,128)(2,1)S(1)} %add_convert_fusion.9), channel_id=1, source_target_pairs={{0,2},{4,0},{8,4},{12,8},{14,12},{10,14},{6,10},{2,6},{1,3},{5,1},... | collective-permute-start | bytes 688136 | tf_op jit(solution)/shard_map/ppermute | solution.py:195
  72.5 2.7 %collective-permute-done.32 = bf16[16,7168]{1,0:T(8,128)(2,1)S(1)} collective-permute-done((bf16[16,7168]{1,0:T(8,128)(2,1)S(1)}, bf16[16,7168]{1,0:T(8,128)(2,1)S(1)}, u32[]{:S(2)}, u32[]{:S(2)}) %collective-permute-start.32) | collective-permute-done | bytes 229408 | tf_op jit(solution)/shard_map/ppermute | solution.py:195
  75.2 1.9 %collective-permute-start.33 = (bf16[16,7168]{1,0:T(8,128)(2,1)S(1)}, bf16[16,7168]{1,0:T(8,128)(2,1)S(1)}, u32[]{:S(2)}, u32[]{:S(2)}) collective-permute-start(bf16[16,7168]{1,0:T(8,128)(2,1)S(1)} %add_convert_fusion.1), channel_id=1, source_target_pairs={{0,2},{4,0},{8,4},{12,8},{14,12},{10,14},{6,10},{2,6},{1,3},{5,1},... | collective-permute-start | bytes 688136 | tf_op jit(solution)/shard_map/ppermute | solution.py:195
  77.4 2.7 %collective-permute-done.16 = bf16[16,7168]{1,0:T(8,128)(2,1)S(1)} collective-permute-done((bf16[16,7168]{1,0:T(8,128)(2,1)S(1)}, bf16[16,7168]{1,0:T(8,128)(2,1)S(1)}, u32[]{:S(2)}, u32[]{:S(2)}) %collective-permute-start.16) | collective-permute-done | bytes 229408 | tf_op jit(solution)/shard_map/ppermute | solution.py:195
  80.1 1.9 %collective-permute-start.17 = (bf16[16,7168]{1,0:T(8,128)(2,1)S(1)}, bf16[16,7168]{1,0:T(8,128)(2,1)S(1)}, u32[]{:S(2)}, u32[]{:S(2)}) collective-permute-start(bf16[16,7168]{1,0:T(8,128)(2,1)S(1)} %add_convert_fusion.8), channel_id=1, source_target_pairs={{0,2},{4,0},{8,4},{12,8},{14,12},{10,14},{6,10},{2,6},{1,3},{5,1},... | collective-permute-start | bytes 688136 | tf_op jit(solution)/shard_map/ppermute | solution.py:195
  82.3 1.5 %collective-permute-done.33 = bf16[16,7168]{1,0:T(8,128)(2,1)S(1)} collective-permute-done((bf16[16,7168]{1,0:T(8,128)(2,1)S(1)}, bf16[16,7168]{1,0:T(8,128)(2,1)S(1)}, u32[]{:S(2)}, u32[]{:S(2)}) %collective-permute-start.33) | collective-permute-done | bytes 229408 | tf_op jit(solution)/shard_map/ppermute | solution.py:195
  83.8 1.7 %collective-permute-done.29 = bf16[16,7168]{1,0:T(8,128)(2,1)S(1)} collective-permute-done((bf16[16,7168]{1,0:T(8,128)(2,1)S(1)}, bf16[16,7168]{1,0:T(8,128)(2,1)S(1)}, u32[]{:S(2)}, u32[]{:S(2)}) %collective-permute-start.29) | collective-permute-done | bytes 229408 | tf_op jit(solution)/shard_map/ppermute | solution.py:192
  85.6 0.7 collective-permute-done.17
  86.2 2.0 %collective-permute-done.13 = bf16[16,7168]{1,0:T(8,128)(2,1)S(1)} collective-permute-done((bf16[16,7168]{1,0:T(8,128)(2,1)S(1)}, bf16[16,7168]{1,0:T(8,128)(2,1)S(1)}, u32[]{:S(2)}, u32[]{:S(2)}) %collective-permute-start.13) | collective-permute-done | bytes 229408 | tf_op jit(solution)/shard_map/ppermute | solution.py:192
  88.3 0.8 pad_maximum_fusion
  (44 shorter events, 1.9 us)
Async XLA Ops:
  0.0 45.9 %collective-permute-start.8 = (bf16[1,7168,512]{2,1,0:T(8,128)(2,1)}, bf16[1,7168,512]{2,1,0:T(8,128)(2,1)S(1)}, u32[]{:S(2)}, u32[]{:S(2)}) collective-permute-start(bf16[1,7168,512]{2,1,0:T(8,128)(2,1)} %param.8), channel_id=1, source_target_pairs={{0,1},{1,0},{2,3},{3,2},{4,5},{5,4},{6,7},{7,6},{8,9},{9,8},{10,11... | collective-permute-start | bytes 22020104 | tf_op jit(solution)/shard_map/ppermute | solution.py:238
  0.5 45.4 %collective-permute-start.9 = (bf16[1,256,7168]{2,1,0:T(8,128)(2,1)}, bf16[1,256,7168]{2,1,0:T(8,128)(2,1)S(1)}, u32[]{:S(2)}, u32[]{:S(2)}) collective-permute-start(bf16[1,256,7168]{2,1,0:T(8,128)(2,1)} %param.9), channel_id=1, source_target_pairs={{0,1},{1,0},{2,3},{3,2},{4,5},{5,4},{6,7},{7,6},{8,9},{9,8},{10,11... | collective-permute-start | bytes 11010056 | tf_op jit(solution)/shard_map/ppermute | solution.py:239
  1.6 9.5 %collective-permute-start.18 = (bf16[16,7168]{1,0:T(8,128)(2,1)S(1)}, bf16[16,7168]{1,0:T(8,128)(2,1)S(1)}, u32[]{:S(2)}, u32[]{:S(2)}) collective-permute-start(bf16[16,7168]{1,0:T(8,128)(2,1)S(1)} %get-tuple-element.35.refs_0_), channel_id=1, source_target_pairs={{0,4},{4,8},{8,12},{12,14},{14,10},{10,6},{6,2},{2,0},{1,5},{5,9},... | collective-permute-start | bytes 688136 | tf_op jit(solution)/shard_map/ppermute | solution.py:192
  4.7 8.4 %collective-permute-start.19 = (bf16[16,7168]{1,0:T(8,128)(2,1)S(1)}, bf16[16,7168]{1,0:T(8,128)(2,1)S(1)}, u32[]{:S(2)}, u32[]{:S(2)}) collective-permute-start(bf16[16,7168]{1,0:T(8,128)(2,1)S(1)} %get-tuple-element.35.refs_0_), channel_id=1, source_target_pairs={{0,2},{4,0},{8,4},{12,8},{14,12},{10,14},{6,10},{2,6},{1,3},{5,1},... | collective-permute-start | bytes 688136 | tf_op jit(solution)/shard_map/ppermute | solution.py:195
  4.7 11.4 %collective-permute-start = (bf16[16,7296]{1,0:T(8,128)(2,1)S(1)}, bf16[16,7296]{1,0:T(8,128)(2,1)S(1)}, u32[]{:S(2)}, u32[]{:S(2)}) collective-permute-start(bf16[16,7296]{1,0:T(8,128)(2,1)S(1)} %get-tuple-element.25.refs_0_.refs_9_), channel_id=1, source_target_pairs={{0,4},{4,8},{8,12},{12,14},{14,10},{10,6},{6,2},{2,0},{1,5},{5,9},... | collective-permute-start | bytes 700424 | tf_op jit(solution)/shard_map/ppermute | solution.py:192
  11.1 7.0 %collective-permute-start.1 = (bf16[16,7296]{1,0:T(8,128)(2,1)S(1)}, bf16[16,7296]{1,0:T(8,128)(2,1)S(1)}, u32[]{:S(2)}, u32[]{:S(2)}) collective-permute-start(bf16[16,7296]{1,0:T(8,128)(2,1)S(1)} %get-tuple-element.25.refs_0_.refs_9_), channel_id=1, source_target_pairs={{0,2},{4,0},{8,4},{12,8},{14,12},{10,14},{6,10},{2,6},{1,3},{5,1},... | collective-permute-start | bytes 700424 | tf_op jit(solution)/shard_map/ppermute | solution.py:195
  13.2 8.5 %collective-permute-start.20 = (bf16[16,7168]{1,0:T(8,128)(2,1)S(1)}, bf16[16,7168]{1,0:T(8,128)(2,1)S(1)}, u32[]{:S(2)}, u32[]{:S(2)}) collective-permute-start(bf16[16,7168]{1,0:T(8,128)(2,1)S(1)} %collective-permute-done.18.refs_1_), channel_id=1, source_target_pairs={{0,4},{4,8},{8,12},{12,14},{14,10},{10,6},{6,2},{2,0},{1,5},{5,9},... | collective-permute-start | bytes 688136 | tf_op jit(solution)/shard_map/ppermute | solution.py:192
  16.1 7.1 %collective-permute-start.21 = (bf16[16,7168]{1,0:T(8,128)(2,1)S(1)}, bf16[16,7168]{1,0:T(8,128)(2,1)S(1)}, u32[]{:S(2)}, u32[]{:S(2)}) collective-permute-start(bf16[16,7168]{1,0:T(8,128)(2,1)S(1)} %collective-permute-done.19.refs_2_), channel_id=1, source_target_pairs={{0,2},{4,0},{8,4},{12,8},{14,12},{10,14},{6,10},{2,6},{1,3},{5,1},... | collective-permute-start | bytes 688136 | tf_op jit(solution)/shard_map/ppermute | solution.py:195
  18.2 8.6 %collective-permute-start.2 = (bf16[16,7296]{1,0:T(8,128)(2,1)S(1)}, bf16[16,7296]{1,0:T(8,128)(2,1)S(1)}, u32[]{:S(2)}, u32[]{:S(2)}) collective-permute-start(bf16[16,7296]{1,0:T(8,128)(2,1)S(1)} %collective-permute-done.refs_1_.refs_10_), channel_id=1, source_target_pairs={{0,4},{4,8},{8,12},{12,14},{14,10},{10,6},{6,2},{2,0},{1,5},{5,9},... | collective-permute-start | bytes 700424 | tf_op jit(solution)/shard_map/ppermute | solution.py:192
  21.6 6.7 %collective-permute-start.3 = (bf16[16,7296]{1,0:T(8,128)(2,1)S(1)}, bf16[16,7296]{1,0:T(8,128)(2,1)S(1)}, u32[]{:S(2)}, u32[]{:S(2)}) collective-permute-start(bf16[16,7296]{1,0:T(8,128)(2,1)S(1)} %collective-permute-done.1.refs_2_.refs_11_), channel_id=1, source_target_pairs={{0,2},{4,0},{8,4},{12,8},{14,12},{10,14},{6,10},{2,6},{1,3},{5,1},... | collective-permute-start | bytes 700424 | tf_op jit(solution)/shard_map/ppermute | solution.py:195
  23.2 8.5 %collective-permute-start.22 = (bf16[16,7168]{1,0:T(8,128)(2,1)S(1)}, bf16[16,7168]{1,0:T(8,128)(2,1)S(1)}, u32[]{:S(2)}, u32[]{:S(2)}) collective-permute-start(bf16[16,7168]{1,0:T(8,128)(2,1)S(1)} %collective-permute-done.20.refs_3_), channel_id=1, source_target_pairs={{0,4},{4,8},{8,12},{12,14},{14,10},{10,6},{6,2},{2,0},{1,5},{5,9},... | collective-permute-start | bytes 688136 | tf_op jit(solution)/shard_map/ppermute | solution.py:192
  26.7 6.7 %collective-permute-start.23 = (bf16[16,7168]{1,0:T(8,128)(2,1)S(1)}, bf16[16,7168]{1,0:T(8,128)(2,1)S(1)}, u32[]{:S(2)}, u32[]{:S(2)}) collective-permute-start(bf16[16,7168]{1,0:T(8,128)(2,1)S(1)} %collective-permute-done.21.refs_4_), channel_id=1, source_target_pairs={{0,2},{4,0},{8,4},{12,8},{14,12},{10,14},{6,10},{2,6},{1,3},{5,1},... | collective-permute-start | bytes 688136 | tf_op jit(solution)/shard_map/ppermute | solution.py:195
  28.3 8.2 %collective-permute-start.4 = (bf16[16,7296]{1,0:T(8,128)(2,1)S(1)}, bf16[16,7296]{1,0:T(8,128)(2,1)S(1)}, u32[]{:S(2)}, u32[]{:S(2)}) collective-permute-start(bf16[16,7296]{1,0:T(8,128)(2,1)S(1)} %collective-permute-done.2.refs_3_.refs_12_), channel_id=1, source_target_pairs={{0,4},{4,8},{8,12},{12,14},{14,10},{10,6},{6,2},{2,0},{1,5},{5,9},... | collective-permute-start | bytes 700424 | tf_op jit(solution)/shard_map/ppermute | solution.py:192
  31.7 6.8 %collective-permute-start.5 = (bf16[16,7296]{1,0:T(8,128)(2,1)S(1)}, bf16[16,7296]{1,0:T(8,128)(2,1)S(1)}, u32[]{:S(2)}, u32[]{:S(2)}) collective-permute-start(bf16[16,7296]{1,0:T(8,128)(2,1)S(1)} %collective-permute-done.3.refs_4_.refs_13_), channel_id=1, source_target_pairs={{0,2},{4,0},{8,4},{12,8},{14,12},{10,14},{6,10},{2,6},{1,3},{5,1},... | collective-permute-start | bytes 700424 | tf_op jit(solution)/shard_map/ppermute | solution.py:195
  33.4 6.2 %collective-permute-start.24 = (bf16[8,7168]{1,0:T(8,128)(2,1)S(1)}, bf16[8,7168]{1,0:T(8,128)(2,1)S(1)}, u32[]{:S(2)}, u32[]{:S(2)}) collective-permute-start(bf16[8,7168]{1,0:T(8,128)(2,1)S(1)} %slice.18), channel_id=1, source_target_pairs={{0,4},{4,8},{8,12},{12,14},{14,10},{10,6},{6,2},{2,0},{1,5},{5,9},... | collective-permute-start | bytes 344072 | tf_op jit(solution)/shard_map/ppermute | solution.py:192
  36.5 9.3 %collective-permute-start.25 = (bf16[8,7168]{1,0:T(8,128)(2,1)S(1)}, bf16[8,7168]{1,0:T(8,128)(2,1)S(1)}, u32[]{:S(2)}, u32[]{:S(2)}) collective-permute-start(bf16[8,7168]{1,0:T(8,128)(2,1)S(1)} %slice.19), channel_id=1, source_target_pairs={{0,2},{4,0},{8,4},{12,8},{14,12},{10,14},{6,10},{2,6},{1,3},{5,1},... | collective-permute-start | bytes 344072 | tf_op jit(solution)/shard_map/ppermute | solution.py:195
  38.5 7.4 %collective-permute-start.6 = (bf16[8,7296]{1,0:T(8,128)(2,1)S(1)}, bf16[8,7296]{1,0:T(8,128)(2,1)S(1)}, u32[]{:S(2)}, u32[]{:S(2)}) collective-permute-start(bf16[8,7296]{1,0:T(8,128)(2,1)S(1)} %slice.16), channel_id=1, source_target_pairs={{0,4},{4,8},{8,12},{12,14},{14,10},{10,6},{6,2},{2,0},{1,5},{5,9},... | collective-permute-start | bytes 350216 | tf_op jit(solution)/shard_map/ppermute | solution.py:192
  39.6 6.3 %collective-permute-start.7 = (bf16[8,7296]{1,0:T(8,128)(2,1)S(1)}, bf16[8,7296]{1,0:T(8,128)(2,1)S(1)}, u32[]{:S(2)}, u32[]{:S(2)}) collective-permute-start(bf16[8,7296]{1,0:T(8,128)(2,1)S(1)} %slice.17), channel_id=1, source_target_pairs={{0,2},{4,0},{8,4},{12,8},{14,12},{10,14},{6,10},{2,6},{1,3},{5,1},... | collective-permute-start | bytes 350216 | tf_op jit(solution)/shard_map/ppermute | solution.py:195
  49.1 7.3 %collective-permute-start.30 = (bf16[8,7168]{1,0:T(8,128)(2,1)S(1)}, bf16[8,7168]{1,0:T(8,128)(2,1)S(1)}, u32[]{:S(2)}, u32[]{:S(2)}) collective-permute-start(bf16[8,7168]{1,0:T(8,128)(2,1)S(1)} %get-tuple-element.41), channel_id=1, source_target_pairs={{0,2},{4,0},{8,4},{12,8},{14,12},{10,14},{6,10},{2,6},{1,3},{5,1},... | collective-permute-start | bytes 344072 | tf_op jit(solution)/shard_map/ppermute | solution.py:195
  51.0 7.4 %collective-permute-start.26 = (bf16[8,7168]{1,0:T(8,128)(2,1)S(1)}, bf16[8,7168]{1,0:T(8,128)(2,1)S(1)}, u32[]{:S(2)}, u32[]{:S(2)}) collective-permute-start(bf16[8,7168]{1,0:T(8,128)(2,1)S(1)} %get-tuple-element.37), channel_id=1, source_target_pairs={{0,4},{4,8},{8,12},{12,14},{14,10},{10,6},{6,2},{2,0},{1,5},{5,9},... | collective-permute-start | bytes 344072 | tf_op jit(solution)/shard_map/ppermute | solution.py:192
  54.4 6.1 %collective-permute-start.14 = (bf16[8,7168]{1,0:T(8,128)(2,1)S(1)}, bf16[8,7168]{1,0:T(8,128)(2,1)S(1)}, u32[]{:S(2)}, u32[]{:S(2)}) collective-permute-start(bf16[8,7168]{1,0:T(8,128)(2,1)S(1)} %get-tuple-element.31), channel_id=1, source_target_pairs={{0,2},{4,0},{8,4},{12,8},{14,12},{10,14},{6,10},{2,6},{1,3},{5,1},... | collective-permute-start | bytes 344072 | tf_op jit(solution)/shard_map/ppermute | solution.py:195
  56.3 6.1 %collective-permute-start.10 = (bf16[8,7168]{1,0:T(8,128)(2,1)S(1)}, bf16[8,7168]{1,0:T(8,128)(2,1)S(1)}, u32[]{:S(2)}, u32[]{:S(2)}) collective-permute-start(bf16[8,7168]{1,0:T(8,128)(2,1)S(1)} %get-tuple-element.27), channel_id=1, source_target_pairs={{0,4},{4,8},{8,12},{12,14},{14,10},{10,6},{6,2},{2,0},{1,5},{5,9},... | collective-permute-start | bytes 344072 | tf_op jit(solution)/shard_map/ppermute | solution.py:192
  56.5 8.9 %collective-permute-start.31 = (bf16[16,7168]{1,0:T(8,128)(2,1)S(1)}, bf16[16,7168]{1,0:T(8,128)(2,1)S(1)}, u32[]{:S(2)}, u32[]{:S(2)}) collective-permute-start(bf16[16,7168]{1,0:T(8,128)(2,1)S(1)} %add_convert_fusion.3), channel_id=1, source_target_pairs={{0,2},{4,0},{8,4},{12,8},{14,12},{10,14},{6,10},{2,6},{1,3},{5,1},... | collective-permute-start | bytes 688136 | tf_op jit(solution)/shard_map/ppermute | solution.py:195
  58.5 8.9 %collective-permute-start.27 = (bf16[16,7168]{1,0:T(8,128)(2,1)S(1)}, bf16[16,7168]{1,0:T(8,128)(2,1)S(1)}, u32[]{:S(2)}, u32[]{:S(2)}) collective-permute-start(bf16[16,7168]{1,0:T(8,128)(2,1)S(1)} %add_convert_fusion.6), channel_id=1, source_target_pairs={{0,4},{4,8},{8,12},{12,14},{14,10},{10,6},{6,2},{2,0},{1,5},{5,9},... | collective-permute-start | bytes 688136 | tf_op jit(solution)/shard_map/ppermute | solution.py:192
  60.5 9.8 %collective-permute-start.15 = (bf16[16,7168]{1,0:T(8,128)(2,1)S(1)}, bf16[16,7168]{1,0:T(8,128)(2,1)S(1)}, u32[]{:S(2)}, u32[]{:S(2)}) collective-permute-start(bf16[16,7168]{1,0:T(8,128)(2,1)S(1)} %add_convert_fusion.10), channel_id=1, source_target_pairs={{0,2},{4,0},{8,4},{12,8},{14,12},{10,14},{6,10},{2,6},{1,3},{5,1},... | collective-permute-start | bytes 688136 | tf_op jit(solution)/shard_map/ppermute | solution.py:195
  62.4 9.8 %collective-permute-start.11 = (bf16[16,7168]{1,0:T(8,128)(2,1)S(1)}, bf16[16,7168]{1,0:T(8,128)(2,1)S(1)}, u32[]{:S(2)}, u32[]{:S(2)}) collective-permute-start(bf16[16,7168]{1,0:T(8,128)(2,1)S(1)} %add_convert_fusion.13), channel_id=1, source_target_pairs={{0,4},{4,8},{8,12},{12,14},{14,10},{10,6},{6,2},{2,0},{1,5},{5,9},... | collective-permute-start | bytes 688136 | tf_op jit(solution)/shard_map/ppermute | solution.py:192
  65.4 9.8 %collective-permute-start.32 = (bf16[16,7168]{1,0:T(8,128)(2,1)S(1)}, bf16[16,7168]{1,0:T(8,128)(2,1)S(1)}, u32[]{:S(2)}, u32[]{:S(2)}) collective-permute-start(bf16[16,7168]{1,0:T(8,128)(2,1)S(1)} %add_convert_fusion.2), channel_id=1, source_target_pairs={{0,2},{4,0},{8,4},{12,8},{14,12},{10,14},{6,10},{2,6},{1,3},{5,1},... | collective-permute-start | bytes 688136 | tf_op jit(solution)/shard_map/ppermute | solution.py:195
  67.4 9.8 %collective-permute-start.28 = (bf16[16,7168]{1,0:T(8,128)(2,1)S(1)}, bf16[16,7168]{1,0:T(8,128)(2,1)S(1)}, u32[]{:S(2)}, u32[]{:S(2)}) collective-permute-start(bf16[16,7168]{1,0:T(8,128)(2,1)S(1)} %add_convert_fusion.5), channel_id=1, source_target_pairs={{0,4},{4,8},{8,12},{12,14},{14,10},{10,6},{6,2},{2,0},{1,5},{5,9},... | collective-permute-start | bytes 688136 | tf_op jit(solution)/shard_map/ppermute | solution.py:192
  70.3 9.8 %collective-permute-start.16 = (bf16[16,7168]{1,0:T(8,128)(2,1)S(1)}, bf16[16,7168]{1,0:T(8,128)(2,1)S(1)}, u32[]{:S(2)}, u32[]{:S(2)}) collective-permute-start(bf16[16,7168]{1,0:T(8,128)(2,1)S(1)} %add_convert_fusion.9), channel_id=1, source_target_pairs={{0,2},{4,0},{8,4},{12,8},{14,12},{10,14},{6,10},{2,6},{1,3},{5,1},... | collective-permute-start | bytes 688136 | tf_op jit(solution)/shard_map/ppermute | solution.py:195
  72.3 9.8 %collective-permute-start.12 = (bf16[16,7168]{1,0:T(8,128)(2,1)S(1)}, bf16[16,7168]{1,0:T(8,128)(2,1)S(1)}, u32[]{:S(2)}, u32[]{:S(2)}) collective-permute-start(bf16[16,7168]{1,0:T(8,128)(2,1)S(1)} %add_convert_fusion.12), channel_id=1, source_target_pairs={{0,4},{4,8},{8,12},{12,14},{14,10},{10,6},{6,2},{2,0},{1,5},{5,9},... | collective-permute-start | bytes 688136 | tf_op jit(solution)/shard_map/ppermute | solution.py:192
  75.2 8.6 %collective-permute-start.33 = (bf16[16,7168]{1,0:T(8,128)(2,1)S(1)}, bf16[16,7168]{1,0:T(8,128)(2,1)S(1)}, u32[]{:S(2)}, u32[]{:S(2)}) collective-permute-start(bf16[16,7168]{1,0:T(8,128)(2,1)S(1)} %add_convert_fusion.1), channel_id=1, source_target_pairs={{0,2},{4,0},{8,4},{12,8},{14,12},{10,14},{6,10},{2,6},{1,3},{5,1},... | collective-permute-start | bytes 688136 | tf_op jit(solution)/shard_map/ppermute | solution.py:195
  77.2 8.3 %collective-permute-start.29 = (bf16[16,7168]{1,0:T(8,128)(2,1)S(1)}, bf16[16,7168]{1,0:T(8,128)(2,1)S(1)}, u32[]{:S(2)}, u32[]{:S(2)}) collective-permute-start(bf16[16,7168]{1,0:T(8,128)(2,1)S(1)} %add_convert_fusion.4), channel_id=1, source_target_pairs={{0,4},{4,8},{8,12},{12,14},{14,10},{10,6},{6,2},{2,0},{1,5},{5,9},... | collective-permute-start | bytes 688136 | tf_op jit(solution)/shard_map/ppermute | solution.py:192
  80.1 6.1 %collective-permute-start.17 = (bf16[16,7168]{1,0:T(8,128)(2,1)S(1)}, bf16[16,7168]{1,0:T(8,128)(2,1)S(1)}, u32[]{:S(2)}, u32[]{:S(2)}) collective-permute-start(bf16[16,7168]{1,0:T(8,128)(2,1)S(1)} %add_convert_fusion.8), channel_id=1, source_target_pairs={{0,2},{4,0},{8,4},{12,8},{14,12},{10,14},{6,10},{2,6},{1,3},{5,1},... | collective-permute-start | bytes 688136 | tf_op jit(solution)/shard_map/ppermute | solution.py:195
  82.1 6.1 %collective-permute-start.13 = (bf16[16,7168]{1,0:T(8,128)(2,1)S(1)}, bf16[16,7168]{1,0:T(8,128)(2,1)S(1)}, u32[]{:S(2)}, u32[]{:S(2)}) collective-permute-start(bf16[16,7168]{1,0:T(8,128)(2,1)S(1)} %add_convert_fusion.11), channel_id=1, source_target_pairs={{0,4},{4,8},{8,12},{12,14},{14,10},{10,6},{6,2},{2,0},{1,5},{5,9},... | collective-permute-start | bytes 688136 | tf_op jit(solution)/shard_map/ppermute | solution.py:192

commit v2 on v1

--- a/solution.py
+++ b/solution.py
@@ -11,6 +11,8 @@
 SUBSETS = 2
 LANES = 128
 ROWS = 128
+DEPTH = 512
+TILE = 512
 
 
 def ring_order(mesh):
@@ -114,7 +116,7 @@
     )(*inputs)
 
 
-def expert_body(subset, node_size, local_count, block_count, side_count, *refs):
+def expert_body(subset, node_size, local_count, block_count, late, side_count, *refs):
     expert_count = node_size * local_count
     expert_total = lax.axis_size("ep") * expert_count
     blocks = refs[:block_count]
@@ -134,11 +136,13 @@
     side_width = side_columns(expert_total)
     side = jnp.concatenate([ref[:, ref.shape[1] - side_width :] for ref in sides], axis=0).astype(jnp.float32)
     lane = lax.broadcasted_iota(jnp.int32, side.shape, 1) - subset * 3 * expert_total
-    depth = 1024 if width % 1024 == 0 else width
     totals = [None] * expert_count
-    for k in range(width // depth):
-        at = slice(k * depth, (k + 1) * depth)
-        x = jnp.concatenate([block[:, at] for block in blocks], axis=0)
+    for k in range(0, width, DEPTH):
+        at = slice(k, k + DEPTH)
+        parts = [block[:, at] for block in blocks[: block_count - late]]
+        if late:
+            parts.append(blocks[-1][:, at])
+        x = jnp.concatenate(parts, axis=0)
         for e in range(expert_count):
             part = jnp.dot(x, ups[e][at, :], preferred_element_type=jnp.float32)
             totals[e] = part if totals[e] is None else totals[e] + part
@@ -146,35 +150,42 @@
     for e, total in enumerate(totals):
         mine = (lane == numbers[e]) | (lane == numbers[e] + expert_total) | (lane == numbers[e] + 2 * expert_total)
         scale = jnp.sum(jnp.where(mine, side, 0.0), axis=1, keepdims=True)
-        hidden.append((scale * (jax.nn.silu(total[:, :inner]) * total[:, inner:])).astype(jnp.bfloat16))
-    tile = 512 if width % 512 == 0 else LANES
-    for n in range(width // tile):
-        at = slice(n * tile, (n + 1) * tile)
+        rounded = (jax.nn.silu(total[:, :inner]) * total[:, inner:]).astype(jnp.bfloat16)
+        hidden.append((scale * rounded.astype(jnp.float32)).astype(jnp.bfloat16))
+    for n in range(0, width, TILE):
+        at = slice(n, n + TILE)
         y = None
         for e in range(expert_count):
             part = jnp.dot(hidden[e], downs[e][:, at], preferred_element_type=jnp.float32)
             y = part if y is None else y + part
         row = 0
-        for out in out_refs:
-            out[:, at] = y[row : row + out.shape[0]].astype(out.dtype)
+        for out in out_refs[: block_count - late]:
+            out[:, at] = y[row : row + out.shape[0]]
             row += out.shape[0]
+        if late:
+            out_refs[-1][:, at] = y[row:].astype(jnp.bfloat16)
 
 
 def side_columns(expert_total):
     return -(-SUBSETS * 3 * expert_total // LANES) * LANES
 
 
-def apply_experts(subset, blocks, sides, dtypes, ups, downs, node_size):
+def apply_experts(subset, blocks, late, sides, ups, downs, node_size):
     inner, width = downs[0].shape
-    rows = sum(block.shape[0] for block in blocks)
+    rows = sum(block.shape[0] for block in (*blocks, *late))
+    out_shape = [jax.ShapeDtypeStruct((block.shape[0], width), jnp.float32) for block in blocks]
+    if late:
+        out_shape += [jax.ShapeDtypeStruct((late[0].shape[0], width), jnp.bfloat16)]
     vmem = pl.BlockSpec(memory_space=pltpu.VMEM)
     weights = [pltpu.with_memory_space_constraint(x, pltpu.VMEM) for x in (*ups, *downs)]
-    inputs = [*blocks, *sides, *weights]
+    inputs = [*blocks, *late, *sides, *weights]
     return pl.pallas_call(
-        functools.partial(expert_body, subset, node_size, len(ups) // node_size, len(blocks), len(sides)),
-        out_shape=[jax.ShapeDtypeStruct((b.shape[0], width), dtype) for b, dtype in zip(blocks, dtypes)],
+        functools.partial(
+            expert_body, subset, node_size, len(ups) // node_size, len(blocks) + len(late), bool(late), len(sides)
+        ),
+        out_shape=out_shape,
         in_specs=[vmem] * len(inputs),
-        out_specs=[vmem] * len(blocks),
+        out_specs=[vmem] * len(out_shape),
         compiler_params=pltpu.CompilerParams(vmem_limit_bytes=12 << 20),
         cost_estimate=pl.CostEstimate(
             flops=6 * rows * width * inner * len(ups), bytes_accessed=rows * width * 6, transcendentals=rows * inner
@@ -194,32 +205,29 @@
     def back(x):
         return lax.ppermute(x, "ep", backward)
 
-    def gather(own):
-        rows = own.shape[0] // 2
+    def gather(own, onward_last):
         left, right = own, own
         blocks = [own]
         for i in range(half_way):
-            if i == half_way - 1:
-                left, right = left[:rows], right[rows:]
-            left = on(left)
-            right = back(right)
-            blocks += [left, right]
+            last = i == half_way - 1
+            if not last or onward_last:
+                left = on(left)
+            if not last or not onward_last:
+                right = back(right)
+            blocks += [left if onward_last else right] if last else [left, right]
         return blocks
 
-    def scatter(sums):
-        left, right = sums[-2:]
-        rows, other = left.shape[0], right.shape[0]
+    def scatter(sums, onward_first):
+        left, right = (sums[-1], None) if onward_first else (None, sums[-1])
         for i in range(half_way):
-            left = on(left)
-            right = back(right)
-            left, right = left.astype(jnp.float32), right.astype(jnp.float32)
-            if i == 0:
-                left = jnp.pad(left, ((0, other), (0, 0)))
-                right = jnp.pad(right, ((rows, 0), (0, 0)))
-            distance = half_way - 1 - i
-            if distance:
-                left = (left + sums[2 * distance]).astype(jnp.bfloat16)
-                right = (right + sums[2 * distance - 1]).astype(jnp.bfloat16)
+            distance = half_way - i
+            if i:
+                left = (sums[2 * distance] if left is None else left + sums[2 * distance]).astype(jnp.bfloat16)
+                right = (sums[2 * distance - 1] if right is None else right + sums[2 * distance - 1]).astype(jnp.bfloat16)
+            if left is not None:
+                left = on(left).astype(jnp.float32)
+            if right is not None:
+                right = back(right).astype(jnp.float32)
         return (sums[0] + left + right).astype(jnp.bfloat16)
 
     def on_device(tokens, expert_ids, gate_weights, gate_up_weight, down_weight):
@@ -228,7 +236,7 @@
         expert_total = count * node_size * local_count
         rows = token_count // SUBSETS
         subsets = pack(tokens, expert_ids, gate_weights, expert_total)
-        gathered = [gather(own) for own in subsets]
+        gathered = [gather(own, s == 0) for s, own in enumerate(subsets)]
         sides = gathered[0]
         ups, downs = [], []
         for shift in range(node_size):
@@ -244,15 +252,19 @@
                     held.append(weight)
         outs = []
         for s in range(SUBSETS):
-            blocks, sums = gathered[s], []
-            dtypes = [jnp.float32] * (len(blocks) - 2) + [jnp.bfloat16] * 2
-            per_call = max(1, ROWS // rows) + 1
-            starts = list(range(len(blocks), 0, -per_call))
-            for end in reversed(starts):
-                at = slice(max(0, end - per_call), end)
-                sums += apply_experts(s, blocks[at], sides[at], dtypes[at], ups, downs, node_size)
-            outs.append(scatter(sums))
-        return jnp.concatenate(outs, axis=0)
+            blocks, late, sums = gathered[s][:-1], gathered[s][-1:], []
+            per_call = max(1, ROWS // rows)
+            total = len(blocks) + 1
+            for first in range(0, total, per_call):
+                end = min(first + per_call, total)
+                sums += apply_experts(
+                    s, blocks[first:end], late if end == total else [], sides[first:end], ups, downs, node_size
+                )
+            outs.append(scatter(sums, s == 0))
+        result = jnp.zeros(tokens.shape, tokens.dtype)
+        for s, out in enumerate(outs):
+            result = lax.optimization_barrier(lax.dynamic_update_slice(result, out, (s * rows, 0)))
+        return result
 
     return on_device
 

time: 89.2 us -> 90.1 us (1.010)
  waiting for transfers between devices: 34.1 us -> 39.3 us
  starting transfers between devices: 40.6 us -> 35.7 us
    ppermute x16 -> x14, waiting for transfers between devices: 19 us -> 23.4 us  [on(): return lax.ppermute(x, 'ep', onward)]
    ppermute x16 -> x14, starting transfers between devices: 13.1 us -> 10.6 us  [on(): return lax.ppermute(x, 'ep', onward)]
    ppermute x16 -> x14, starting transfers between devices: 27 us -> 24.6 us  [back(): return lax.ppermute(x, 'ep', backward)]
    ppermute x16 -> x14, waiting for transfers between devices: 15.1 us -> 15.9 us  [back(): return lax.ppermute(x, 'ep', backward)]
  transfers between devices with their start and end apart: 34 -> 30, of which waited for: 17 -> 16; matrix products, arithmetic and copies ran while one was open for 1% -> 1% of each run, Pallas kernels for 11% -> 11%
where the time goes in v2:
time: 90.1 us; the launch traced here: 89.9 us
  waiting for transfers between devices  39.3 us (44%)
  starting transfers between devices  35.7 us (40%)
  Pallas kernels  12.7 us (14%)
  other arithmetic  1.34 us (1%)
    ppermute x14, starting transfers between devices, back(): return lax.ppermute(x, 'ep', backward)  24.6 us
    ppermute x14, waiting for transfers between devices, on(): return lax.ppermute(x, 'ep', onward)  23.4 us
    ppermute x14, waiting for transfers between devices, back(): return lax.ppermute(x, 'ep', backward)  15.9 us
    ppermute x14, starting transfers between devices, on(): return lax.ppermute(x, 'ep', onward)  10.6 us
    pallas_call x2, Pallas kernels, apply_experts(): pl.pallas_call(functools.partial(expert_body, subset, node_size, len(ups)...  6.32 us
    pallas_call x2, Pallas kernels, resident(): pl.pallas_call(body, out_shape=pltpu.VMEM(x.shape, x.dtype), in_specs=[pl...  5.23 us
  transfers between devices with their start and end apart: 30, of which 16 were waited for; matrix products, arithmetic and copies ran while one was open for 1% of the time, Pallas kernels for 11%

profile of v2, /device:TPU:0, one launch (start us, length us, event | category | flops | bytes accessed | tf_op | source)
XLA Modules:
  0.0 89.9 jit_solution(15641846564681302953)
XLA Ops:
  0.0 0.5 collective-permute-start.7
  0.5 1.1 %shard_map.55 = (bf16[16,7296]{1,0:T(8,128)(2,1)S(1)}, bf16[16,7168]{1,0:T(8,128)(2,1)S(1)}) custom-call(s32[8,32]{1,0:T(8,128)} %bitcast.12, f32[8,32]{1,0:T(8,128)} %bitcast.13, bf16[32,7168]{1,0:T(8,128)(2,1)} %tokens_ref.1), custom_call_target="tpu_custom_call" | custom-call | tf_op jit(solution)/shard_map/pallas_call | solution.py:102
  1.6 3.0 %collective-permute-start.17 = (bf16[16,7168]{1,0:T(8,128)(2,1)S(1)}, bf16[16,7168]{1,0:T(8,128)(2,1)S(1)}, u32[]{:S(2)}, u32[]{:S(2)}) collective-permute-start(bf16[16,7168]{1,0:T(8,128)(2,1)S(1)} %get-tuple-element.32.refs_0_), channel_id=1, source_target_pairs={{0,2},{4,0},{8,4},{12,8},{14,12},{10,14},{6,10},{2,6},{1,3},{5,1},... | collective-permute-start | bytes 688136 | tf_op jit(solution)/shard_map/ppermute | solution.py:206
  4.8 2.0 %collective-permute-start = (bf16[16,7296]{1,0:T(8,128)(2,1)S(1)}, bf16[16,7296]{1,0:T(8,128)(2,1)S(1)}, u32[]{:S(2)}, u32[]{:S(2)}) collective-permute-start(bf16[16,7296]{1,0:T(8,128)(2,1)S(1)} %get-tuple-element.23.refs_0_.refs_8_), channel_id=1, source_target_pairs={{0,4},{4,8},{8,12},{12,14},{14,10},{10,6},{6,2},{2,0},{1,5},{5,9},... | collective-permute-start | bytes 700424 | tf_op jit(solution)/shard_map/ppermute | solution.py:203
  6.8 3.7 %collective-permute-done.17.refs_2_ = bf16[16,7168]{1,0:T(8,128)(2,1)S(1)} collective-permute-done((bf16[16,7168]{1,0:T(8,128)(2,1)S(1)}, bf16[16,7168]{1,0:T(8,128)(2,1)S(1)}, u32[]{:S(2)}, u32[]{:S(2)}) %collective-permute-start.17) | collective-permute-done | bytes 229408 | tf_op jit(solution)/shard_map/ppermute | solution.py:206
  10.5 1.7 %collective-permute-start.1 = (bf16[16,7296]{1,0:T(8,128)(2,1)S(1)}, bf16[16,7296]{1,0:T(8,128)(2,1)S(1)}, u32[]{:S(2)}, u32[]{:S(2)}) collective-permute-start(bf16[16,7296]{1,0:T(8,128)(2,1)S(1)} %get-tuple-element.23.refs_0_.refs_8_), channel_id=1, source_target_pairs={{0,2},{4,0},{8,4},{12,8},{14,12},{10,14},{6,10},{2,6},{1,3},{5,1},... | collective-permute-start | bytes 700424 | tf_op jit(solution)/shard_map/ppermute | solution.py:206
  12.2 1.0 %collective-permute-done.16.refs_1_ = bf16[16,7168]{1,0:T(8,128)(2,1)S(1)} collective-permute-done((bf16[16,7168]{1,0:T(8,128)(2,1)S(1)}, bf16[16,7168]{1,0:T(8,128)(2,1)S(1)}, u32[]{:S(2)}, u32[]{:S(2)}) %collective-permute-start.16) | collective-permute-done | bytes 229408 | tf_op jit(solution)/shard_map/ppermute | solution.py:203
  13.2 1.6 %collective-permute-start.19 = (bf16[16,7168]{1,0:T(8,128)(2,1)S(1)}, bf16[16,7168]{1,0:T(8,128)(2,1)S(1)}, u32[]{:S(2)}, u32[]{:S(2)}) collective-permute-start(bf16[16,7168]{1,0:T(8,128)(2,1)S(1)} %collective-permute-done.17.refs_2_), channel_id=1, source_target_pairs={{0,2},{4,0},{8,4},{12,8},{14,12},{10,14},{6,10},{2,6},{1,3},{5,1},... | collective-permute-start | bytes 688136 | tf_op jit(solution)/shard_map/ppermute | solution.py:206
  14.7 2.2 %collective-permute-done.refs_1_.refs_9_ = bf16[16,7296]{1,0:T(8,128)(2,1)S(1)} collective-permute-done((bf16[16,7296]{1,0:T(8,128)(2,1)S(1)}, bf16[16,7296]{1,0:T(8,128)(2,1)S(1)}, u32[]{:S(2)}, u32[]{:S(2)}) %collective-permute-start) | collective-permute-done | bytes 233504 | tf_op jit(solution)/shard_map/ppermute | solution.py:203
  16.9 0.4 collective-permute-start.2
  17.3 1.8 %collective-permute-done.1.refs_2_.refs_10_ = bf16[16,7296]{1,0:T(8,128)(2,1)S(1)} collective-permute-done((bf16[16,7296]{1,0:T(8,128)(2,1)S(1)}, bf16[16,7296]{1,0:T(8,128)(2,1)S(1)}, u32[]{:S(2)}, u32[]{:S(2)}) %collective-permute-start.1) | collective-permute-done | bytes 233504 | tf_op jit(solution)/shard_map/ppermute | solution.py:206
  19.1 1.7 %collective-permute-start.3 = (bf16[16,7296]{1,0:T(8,128)(2,1)S(1)}, bf16[16,7296]{1,0:T(8,128)(2,1)S(1)}, u32[]{:S(2)}, u32[]{:S(2)}) collective-permute-start(bf16[16,7296]{1,0:T(8,128)(2,1)S(1)} %collective-permute-done.1.refs_2_.refs_10_), channel_id=1, source_target_pairs={{0,2},{4,0},{8,4},{12,8},{14,12},{10,14},{6,10},{2,6},{1,3},{5,1},... | collective-permute-start | bytes 700424 | tf_op jit(solution)/shard_map/ppermute | solution.py:206
  20.8 3.2 %collective-permute-done.19.refs_4_ = bf16[16,7168]{1,0:T(8,128)(2,1)S(1)} collective-permute-done((bf16[16,7168]{1,0:T(8,128)(2,1)S(1)}, bf16[16,7168]{1,0:T(8,128)(2,1)S(1)}, u32[]{:S(2)}, u32[]{:S(2)}) %collective-permute-start.19) | collective-permute-done | bytes 229408 | tf_op jit(solution)/shard_map/ppermute | solution.py:206
  24.0 1.7 %collective-permute-start.18 = (bf16[16,7168]{1,0:T(8,128)(2,1)S(1)}, bf16[16,7168]{1,0:T(8,128)(2,1)S(1)}, u32[]{:S(2)}, u32[]{:S(2)}) collective-permute-start(bf16[16,7168]{1,0:T(8,128)(2,1)S(1)} %collective-permute-done.16.refs_1_), channel_id=1, source_target_pairs={{0,4},{4,8},{8,12},{12,14},{14,10},{10,6},{6,2},{2,0},{1,5},{5,9},... | collective-permute-start | bytes 688136 | tf_op jit(solution)/shard_map/ppermute | solution.py:203
  25.7 1.6 %collective-permute-start.4 = (bf16[16,7296]{1,0:T(8,128)(2,1)S(1)}, bf16[16,7296]{1,0:T(8,128)(2,1)S(1)}, u32[]{:S(2)}, u32[]{:S(2)}) collective-permute-start(bf16[16,7296]{1,0:T(8,128)(2,1)S(1)} %collective-permute-done.2.refs_3_.refs_11_), channel_id=1, source_target_pairs={{0,4},{4,8},{8,12},{12,14},{14,10},{10,6},{6,2},{2,0},{1,5},{5,9},... | collective-permute-start | bytes 700424 | tf_op jit(solution)/shard_map/ppermute | solution.py:203
  27.3 4.9 %collective-permute-done.18.refs_3_ = bf16[16,7168]{1,0:T(8,128)(2,1)S(1)} collective-permute-done((bf16[16,7168]{1,0:T(8,128)(2,1)S(1)}, bf16[16,7168]{1,0:T(8,128)(2,1)S(1)}, u32[]{:S(2)}, u32[]{:S(2)}) %collective-permute-start.18) | collective-permute-done | bytes 229408 | tf_op jit(solution)/shard_map/ppermute | solution.py:203
  32.2 1.1 %collective-permute-start.21 = (bf16[16,7168]{1,0:T(8,128)(2,1)S(1)}, bf16[16,7168]{1,0:T(8,128)(2,1)S(1)}, u32[]{:S(2)}, u32[]{:S(2)}) collective-permute-start(bf16[16,7168]{1,0:T(8,128)(2,1)S(1)} %collective-permute-done.19.refs_4_), channel_id=1, source_target_pairs={{0,2},{4,0},{8,4},{12,8},{14,12},{10,14},{6,10},{2,6},{1,3},{5,1},... | collective-permute-start | bytes 688136 | tf_op jit(solution)/shard_map/ppermute | solution.py:206
  33.3 0.9 %collective-permute-start.20 = (bf16[16,7168]{1,0:T(8,128)(2,1)S(1)}, bf16[16,7168]{1,0:T(8,128)(2,1)S(1)}, u32[]{:S(2)}, u32[]{:S(2)}) collective-permute-start(bf16[16,7168]{1,0:T(8,128)(2,1)S(1)} %collective-permute-done.18.refs_3_), channel_id=1, source_target_pairs={{0,4},{4,8},{8,12},{12,14},{14,10},{10,6},{6,2},{2,0},{1,5},{5,9},... | collective-permute-start | bytes 688136 | tf_op jit(solution)/shard_map/ppermute | solution.py:203
  34.2 6.1 %collective-permute-done.21.refs_6_ = bf16[16,7168]{1,0:T(8,128)(2,1)S(1)} collective-permute-done((bf16[16,7168]{1,0:T(8,128)(2,1)S(1)}, bf16[16,7168]{1,0:T(8,128)(2,1)S(1)}, u32[]{:S(2)}, u32[]{:S(2)}) %collective-permute-start.21) | collective-permute-done | bytes 229408 | tf_op jit(solution)/shard_map/ppermute | solution.py:206
  40.3 1.1 %collective-permute-start.5 = (bf16[16,7296]{1,0:T(8,128)(2,1)S(1)}, bf16[16,7296]{1,0:T(8,128)(2,1)S(1)}, u32[]{:S(2)}, u32[]{:S(2)}) collective-permute-start(bf16[16,7296]{1,0:T(8,128)(2,1)S(1)} %collective-permute-done.3.refs_4_.refs_12_), channel_id=1, source_target_pairs={{0,2},{4,0},{8,4},{12,8},{14,12},{10,14},{6,10},{2,6},{1,3},{5,1},... | collective-permute-start | bytes 700424 | tf_op jit(solution)/shard_map/ppermute | solution.py:206
  41.5 1.6 %collective-permute-start.22 = (bf16[16,7168]{1,0:T(8,128)(2,1)S(1)}, bf16[16,7168]{1,0:T(8,128)(2,1)S(1)}, u32[]{:S(2)}, u32[]{:S(2)}) collective-permute-start(bf16[16,7168]{1,0:T(8,128)(2,1)S(1)} %collective-permute-done.21.refs_6_), channel_id=1, source_target_pairs={{0,2},{4,0},{8,4},{12,8},{14,12},{10,14},{6,10},{2,6},{1,3},{5,1},... | collective-permute-start | bytes 688136 | tf_op jit(solution)/shard_map/ppermute | solution.py:206
  43.0 0.4 collective-permute-start.6
  43.5 2.1 %shard_map.57.refs_18_ = bf16[256,7168]{1,0:T(8,128)(2,1)S(1)} custom-call(bf16[256,7168]{1,0:T(8,128)(2,1)} %bitcast.11), custom_call_target="tpu_custom_call" | custom-call | flops 917504000 | bytes 7340032 | tf_op jit(solution)/shard_map/pallas_call | solution.py:52
  45.5 3.2 %shard_map.56.refs_16_ = bf16[7168,512]{1,0:T(8,128)(2,1)S(1)} custom-call(bf16[7168,512]{1,0:T(8,128)(2,1)} %bitcast.10), custom_call_target="tpu_custom_call" | custom-call | flops 1835008000 | bytes 14680064 | tf_op jit(solution)/shard_map/pallas_call | solution.py:52
  48.7 0.8 collective-permute-done.22.refs_7_
  49.6 1.1 %collective-permute-done.6.refs_7_.refs_15_ = bf16[16,7296]{1,0:T(8,128)(2,1)S(1)} collective-permute-done((bf16[16,7296]{1,0:T(8,128)(2,1)S(1)}, bf16[16,7296]{1,0:T(8,128)(2,1)S(1)}, u32[]{:S(2)}, u32[]{:S(2)}) %collective-permute-start.6) | collective-permute-done | bytes 233504 | tf_op jit(solution)/shard_map/ppermute | solution.py:203
  50.7 3.1 %shard_map.59 = (f32[16,7168]{1,0:T(8,128)S(1)}, f32[16,7168]{1,0:T(8,128)S(1)}, f32[16,7168]{1,0:T(8,128)S(1)}, f32[16,7168]{1,0:T(8,128)S(1)}, f32[16,7168]{1,...) custom-call(bf16[16,7168]{1,0:T(8,128)(2,1)S(1)} %get-tuple-element.32.refs_0_, ...), custom_call_target="tpu_custom_call" | custom-call | flops 2818572288 | bytes 5505024 | tf_op jit(solution)/shard_map/pallas_call | solution.py:182
  53.9 0.9 collective-permute-start.23
  54.8 1.9 %collective-permute-start.26 = (bf16[16,7168]{1,0:T(8,128)(2,1)S(1)}, bf16[16,7168]{1,0:T(8,128)(2,1)S(1)}, u32[]{:S(2)}, u32[]{:S(2)}) collective-permute-start(bf16[16,7168]{1,0:T(8,128)(2,1)S(1)} %get-tuple-element.37), channel_id=1, source_target_pairs={{0,2},{4,0},{8,4},{12,8},{14,12},{10,14},{6,10},{2,6},{1,3},{5,1},... | collective-permute-start | bytes 688136 | tf_op jit(solution)/shard_map/ppermute | solution.py:206
  56.7 3.2 %shard_map.58 = (f32[16,7168]{1,0:T(8,128)S(1)}, f32[16,7168]{1,0:T(8,128)S(1)}, f32[16,7168]{1,0:T(8,128)S(1)}, f32[16,7168]{1,0:T(8,128)S(1)}, f32[16,7168]{1,...) custom-call(bf16[16,7296]{1,0:T(8,128)(2,1)S(1)} %get-tuple-element.23.refs_0_.refs_8_,, ...), custom_call_target="tpu_custom_call" | custom-call | flops 2818572288 | bytes 5505024 | tf_op jit(solution)/shard_map/pallas_call | solution.py:182
  59.9 0.4 collective-permute-start.9
  60.3 1.8 %collective-permute-start.13 = (bf16[16,7168]{1,0:T(8,128)(2,1)S(1)}, bf16[16,7168]{1,0:T(8,128)(2,1)S(1)}, u32[]{:S(2)}, u32[]{:S(2)}) collective-permute-start(bf16[16,7168]{1,0:T(8,128)(2,1)S(1)} %convert_element_type.91), channel_id=1, source_target_pairs={{0,2},{4,0},{8,4},{12,8},{14,12},{10,14},{6,10},{2,6},{1,3},{5,1},... | collective-permute-start | bytes 688136 | tf_op jit(solution)/shard_map/ppermute | solution.py:206
  62.1 0.9 %collective-permute-done.23 = bf16[16,7168]{1,0:T(8,128)(2,1)S(1)} collective-permute-done((bf16[16,7168]{1,0:T(8,128)(2,1)S(1)}, bf16[16,7168]{1,0:T(8,128)(2,1)S(1)}, u32[]{:S(2)}, u32[]{:S(2)}) %collective-permute-start.23) | collective-permute-done | bytes 229408 | tf_op jit(solution)/shard_map/ppermute | solution.py:203
  63.6 1.9 %collective-permute-start.27 = (bf16[16,7168]{1,0:T(8,128)(2,1)S(1)}, bf16[16,7168]{1,0:T(8,128)(2,1)S(1)}, u32[]{:S(2)}, u32[]{:S(2)}) collective-permute-start(bf16[16,7168]{1,0:T(8,128)(2,1)S(1)} %add_convert_fusion.3), channel_id=1, source_target_pairs={{0,2},{4,0},{8,4},{12,8},{14,12},{10,14},{6,10},{2,6},{1,3},{5,1},... | collective-permute-start | bytes 688136 | tf_op jit(solution)/shard_map/ppermute | solution.py:206
  65.5 3.0 %collective-permute-done.9 = bf16[16,7168]{1,0:T(8,128)(2,1)S(1)} collective-permute-done((bf16[16,7168]{1,0:T(8,128)(2,1)S(1)}, bf16[16,7168]{1,0:T(8,128)(2,1)S(1)}, u32[]{:S(2)}, u32[]{:S(2)}) %collective-permute-start.9) | collective-permute-done | bytes 229408 | tf_op jit(solution)/shard_map/ppermute | solution.py:203
  68.6 0.3 collective-permute-start.10
  68.9 1.8 %collective-permute-start.14 = (bf16[16,7168]{1,0:T(8,128)(2,1)S(1)}, bf16[16,7168]{1,0:T(8,128)(2,1)S(1)}, u32[]{:S(2)}, u32[]{:S(2)}) collective-permute-start(bf16[16,7168]{1,0:T(8,128)(2,1)S(1)} %add_convert_fusion.8), channel_id=1, source_target_pairs={{0,2},{4,0},{8,4},{12,8},{14,12},{10,14},{6,10},{2,6},{1,3},{5,1},... | collective-permute-start | bytes 688136 | tf_op jit(solution)/shard_map/ppermute | solution.py:206
  70.8 1.5 %collective-permute-done.24 = bf16[16,7168]{1,0:T(8,128)(2,1)S(1)} collective-permute-done((bf16[16,7168]{1,0:T(8,128)(2,1)S(1)}, bf16[16,7168]{1,0:T(8,128)(2,1)S(1)}, u32[]{:S(2)}, u32[]{:S(2)}) %collective-permute-start.24) | collective-permute-done | bytes 229408 | tf_op jit(solution)/shard_map/ppermute | solution.py:203
  72.3 0.7 collective-permute-start.25
  73.0 1.5 %collective-permute-start.28 = (bf16[16,7168]{1,0:T(8,128)(2,1)S(1)}, bf16[16,7168]{1,0:T(8,128)(2,1)S(1)}, u32[]{:S(2)}, u32[]{:S(2)}) collective-permute-start(bf16[16,7168]{1,0:T(8,128)(2,1)S(1)} %add_convert_fusion.2), channel_id=1, source_target_pairs={{0,2},{4,0},{8,4},{12,8},{14,12},{10,14},{6,10},{2,6},{1,3},{5,1},... | collective-permute-start | bytes 688136 | tf_op jit(solution)/shard_map/ppermute | solution.py:206
  74.4 1.1 %collective-permute-done.10 = bf16[16,7168]{1,0:T(8,128)(2,1)S(1)} collective-permute-done((bf16[16,7168]{1,0:T(8,128)(2,1)S(1)}, bf16[16,7168]{1,0:T(8,128)(2,1)S(1)}, u32[]{:S(2)}, u32[]{:S(2)}) %collective-permute-start.10) | collective-permute-done | bytes 229408 | tf_op jit(solution)/shard_map/ppermute | solution.py:203
  76.0 2.3 %collective-permute-start.15 = (bf16[16,7168]{1,0:T(8,128)(2,1)S(1)}, bf16[16,7168]{1,0:T(8,128)(2,1)S(1)}, u32[]{:S(2)}, u32[]{:S(2)}) collective-permute-start(bf16[16,7168]{1,0:T(8,128)(2,1)S(1)} %add_convert_fusion.7), channel_id=1, source_target_pairs={{0,2},{4,0},{8,4},{12,8},{14,12},{10,14},{6,10},{2,6},{1,3},{5,1},... | collective-permute-start | bytes 688136 | tf_op jit(solution)/shard_map/ppermute | solution.py:206
  78.3 3.9 %collective-permute-done.11 = bf16[16,7168]{1,0:T(8,128)(2,1)S(1)} collective-permute-done((bf16[16,7168]{1,0:T(8,128)(2,1)S(1)}, bf16[16,7168]{1,0:T(8,128)(2,1)S(1)}, u32[]{:S(2)}, u32[]{:S(2)}) %collective-permute-start.11) | collective-permute-done | bytes 229408 | tf_op jit(solution)/shard_map/ppermute | solution.py:203
  82.2 0.6 collective-permute-start.12
  82.8 1.6 %collective-permute-start.29 = (bf16[16,7168]{1,0:T(8,128)(2,1)S(1)}, bf16[16,7168]{1,0:T(8,128)(2,1)S(1)}, u32[]{:S(2)}, u32[]{:S(2)}) collective-permute-start(bf16[16,7168]{1,0:T(8,128)(2,1)S(1)} %add_convert_fusion.1), channel_id=1, source_target_pairs={{0,2},{4,0},{8,4},{12,8},{14,12},{10,14},{6,10},{2,6},{1,3},{5,1},... | collective-permute-start | bytes 688136 | tf_op jit(solution)/shard_map/ppermute | solution.py:206
  84.4 3.9 %collective-permute-done.12 = bf16[16,7168]{1,0:T(8,128)(2,1)S(1)} collective-permute-done((bf16[16,7168]{1,0:T(8,128)(2,1)S(1)}, bf16[16,7168]{1,0:T(8,128)(2,1)S(1)}, u32[]{:S(2)}, u32[]{:S(2)}) %collective-permute-start.12) | collective-permute-done | bytes 229408 | tf_op jit(solution)/shard_map/ppermute | solution.py:203
  88.3 0.8 dynamic_update_slice.6
  89.1 0.8 fusion
  (32 shorter events, 1.5 us)
Async XLA Ops:
  0.0 50.7 %collective-permute-start.7 = (bf16[1,7168,512]{2,1,0:T(8,128)(2,1)}, bf16[1,7168,512]{2,1,0:T(8,128)(2,1)S(1)}, u32[]{:S(2)}, u32[]{:S(2)}) collective-permute-start(bf16[1,7168,512]{2,1,0:T(8,128)(2,1)} %param.8), channel_id=1, source_target_pairs={{0,1},{1,0},{2,3},{3,2},{4,5},{5,4},{6,7},{7,6},{8,9},{9,8},{10,11... | collective-permute-start | bytes 22020104 | tf_op jit(solution)/shard_map/ppermute | solution.py:246
  0.5 50.2 %collective-permute-start.8 = (bf16[1,256,7168]{2,1,0:T(8,128)(2,1)}, bf16[1,256,7168]{2,1,0:T(8,128)(2,1)S(1)}, u32[]{:S(2)}, u32[]{:S(2)}) collective-permute-start(bf16[1,256,7168]{2,1,0:T(8,128)(2,1)} %param.9), channel_id=1, source_target_pairs={{0,1},{1,0},{2,3},{3,2},{4,5},{5,4},{6,7},{7,6},{8,9},{9,8},{10,11... | collective-permute-start | bytes 11010056 | tf_op jit(solution)/shard_map/ppermute | solution.py:247
  1.6 8.9 %collective-permute-start.17 = (bf16[16,7168]{1,0:T(8,128)(2,1)S(1)}, bf16[16,7168]{1,0:T(8,128)(2,1)S(1)}, u32[]{:S(2)}, u32[]{:S(2)}) collective-permute-start(bf16[16,7168]{1,0:T(8,128)(2,1)S(1)} %get-tuple-element.32.refs_0_), channel_id=1, source_target_pairs={{0,2},{4,0},{8,4},{12,8},{14,12},{10,14},{6,10},{2,6},{1,3},{5,1},... | collective-permute-start | bytes 688136 | tf_op jit(solution)/shard_map/ppermute | solution.py:206
  4.7 8.5 %collective-permute-start.16 = (bf16[16,7168]{1,0:T(8,128)(2,1)S(1)}, bf16[16,7168]{1,0:T(8,128)(2,1)S(1)}, u32[]{:S(2)}, u32[]{:S(2)}) collective-permute-start(bf16[16,7168]{1,0:T(8,128)(2,1)S(1)} %get-tuple-element.32.refs_0_), channel_id=1, source_target_pairs={{0,4},{4,8},{8,12},{12,14},{14,10},{10,6},{6,2},{2,0},{1,5},{5,9},... | collective-permute-start | bytes 688136 | tf_op jit(solution)/shard_map/ppermute | solution.py:203
  4.8 12.1 %collective-permute-start = (bf16[16,7296]{1,0:T(8,128)(2,1)S(1)}, bf16[16,7296]{1,0:T(8,128)(2,1)S(1)}, u32[]{:S(2)}, u32[]{:S(2)}) collective-permute-start(bf16[16,7296]{1,0:T(8,128)(2,1)S(1)} %get-tuple-element.23.refs_0_.refs_8_), channel_id=1, source_target_pairs={{0,4},{4,8},{8,12},{12,14},{14,10},{10,6},{6,2},{2,0},{1,5},{5,9},... | collective-permute-start | bytes 700424 | tf_op jit(solution)/shard_map/ppermute | solution.py:203
  10.5 8.6 %collective-permute-start.1 = (bf16[16,7296]{1,0:T(8,128)(2,1)S(1)}, bf16[16,7296]{1,0:T(8,128)(2,1)S(1)}, u32[]{:S(2)}, u32[]{:S(2)}) collective-permute-start(bf16[16,7296]{1,0:T(8,128)(2,1)S(1)} %get-tuple-element.23.refs_0_.refs_8_), channel_id=1, source_target_pairs={{0,2},{4,0},{8,4},{12,8},{14,12},{10,14},{6,10},{2,6},{1,3},{5,1},... | collective-permute-start | bytes 700424 | tf_op jit(solution)/shard_map/ppermute | solution.py:206
  13.2 10.8 %collective-permute-start.19 = (bf16[16,7168]{1,0:T(8,128)(2,1)S(1)}, bf16[16,7168]{1,0:T(8,128)(2,1)S(1)}, u32[]{:S(2)}, u32[]{:S(2)}) collective-permute-start(bf16[16,7168]{1,0:T(8,128)(2,1)S(1)} %collective-permute-done.17.refs_2_), channel_id=1, source_target_pairs={{0,2},{4,0},{8,4},{12,8},{14,12},{10,14},{6,10},{2,6},{1,3},{5,1},... | collective-permute-start | bytes 688136 | tf_op jit(solution)/shard_map/ppermute | solution.py:206
  16.9 8.8 %collective-permute-start.2 = (bf16[16,7296]{1,0:T(8,128)(2,1)S(1)}, bf16[16,7296]{1,0:T(8,128)(2,1)S(1)}, u32[]{:S(2)}, u32[]{:S(2)}) collective-permute-start(bf16[16,7296]{1,0:T(8,128)(2,1)S(1)} %collective-permute-done.refs_1_.refs_9_), channel_id=1, source_target_pairs={{0,4},{4,8},{8,12},{12,14},{14,10},{10,6},{6,2},{2,0},{1,5},{5,9},... | collective-permute-start | bytes 700424 | tf_op jit(solution)/shard_map/ppermute | solution.py:203
  19.1 14.3 %collective-permute-start.3 = (bf16[16,7296]{1,0:T(8,128)(2,1)S(1)}, bf16[16,7296]{1,0:T(8,128)(2,1)S(1)}, u32[]{:S(2)}, u32[]{:S(2)}) collective-permute-start(bf16[16,7296]{1,0:T(8,128)(2,1)S(1)} %collective-permute-done.1.refs_2_.refs_10_), channel_id=1, source_target_pairs={{0,2},{4,0},{8,4},{12,8},{14,12},{10,14},{6,10},{2,6},{1,3},{5,1},... | collective-permute-start | bytes 700424 | tf_op jit(solution)/shard_map/ppermute | solution.py:206
  24.0 8.2 %collective-permute-start.18 = (bf16[16,7168]{1,0:T(8,128)(2,1)S(1)}, bf16[16,7168]{1,0:T(8,128)(2,1)S(1)}, u32[]{:S(2)}, u32[]{:S(2)}) collective-permute-start(bf16[16,7168]{1,0:T(8,128)(2,1)S(1)} %collective-permute-done.16.refs_1_), channel_id=1, source_target_pairs={{0,4},{4,8},{8,12},{12,14},{14,10},{10,6},{6,2},{2,0},{1,5},{5,9},... | collective-permute-start | bytes 688136 | tf_op jit(solution)/shard_map/ppermute | solution.py:203
  25.7 17.3 %collective-permute-start.4 = (bf16[16,7296]{1,0:T(8,128)(2,1)S(1)}, bf16[16,7296]{1,0:T(8,128)(2,1)S(1)}, u32[]{:S(2)}, u32[]{:S(2)}) collective-permute-start(bf16[16,7296]{1,0:T(8,128)(2,1)S(1)} %collective-permute-done.2.refs_3_.refs_11_), channel_id=1, source_target_pairs={{0,4},{4,8},{8,12},{12,14},{14,10},{10,6},{6,2},{2,0},{1,5},{5,9},... | collective-permute-start | bytes 700424 | tf_op jit(solution)/shard_map/ppermute | solution.py:203
  32.2 8.1 %collective-permute-start.21 = (bf16[16,7168]{1,0:T(8,128)(2,1)S(1)}, bf16[16,7168]{1,0:T(8,128)(2,1)S(1)}, u32[]{:S(2)}, u32[]{:S(2)}) collective-permute-start(bf16[16,7168]{1,0:T(8,128)(2,1)S(1)} %collective-permute-done.19.refs_4_), channel_id=1, source_target_pairs={{0,2},{4,0},{8,4},{12,8},{14,12},{10,14},{6,10},{2,6},{1,3},{5,1},... | collective-permute-start | bytes 688136 | tf_op jit(solution)/shard_map/ppermute | solution.py:206
  33.3 8.1 %collective-permute-start.20 = (bf16[16,7168]{1,0:T(8,128)(2,1)S(1)}, bf16[16,7168]{1,0:T(8,128)(2,1)S(1)}, u32[]{:S(2)}, u32[]{:S(2)}) collective-permute-start(bf16[16,7168]{1,0:T(8,128)(2,1)S(1)} %collective-permute-done.18.refs_3_), channel_id=1, source_target_pairs={{0,4},{4,8},{8,12},{12,14},{14,10},{10,6},{6,2},{2,0},{1,5},{5,9},... | collective-permute-start | bytes 688136 | tf_op jit(solution)/shard_map/ppermute | solution.py:203
  40.3 8.4 %collective-permute-start.5 = (bf16[16,7296]{1,0:T(8,128)(2,1)S(1)}, bf16[16,7296]{1,0:T(8,128)(2,1)S(1)}, u32[]{:S(2)}, u32[]{:S(2)}) collective-permute-start(bf16[16,7296]{1,0:T(8,128)(2,1)S(1)} %collective-permute-done.3.refs_4_.refs_12_), channel_id=1, source_target_pairs={{0,2},{4,0},{8,4},{12,8},{14,12},{10,14},{6,10},{2,6},{1,3},{5,1},... | collective-permute-start | bytes 700424 | tf_op jit(solution)/shard_map/ppermute | solution.py:206
  41.5 8.1 %collective-permute-start.22 = (bf16[16,7168]{1,0:T(8,128)(2,1)S(1)}, bf16[16,7168]{1,0:T(8,128)(2,1)S(1)}, u32[]{:S(2)}, u32[]{:S(2)}) collective-permute-start(bf16[16,7168]{1,0:T(8,128)(2,1)S(1)} %collective-permute-done.21.refs_6_), channel_id=1, source_target_pairs={{0,2},{4,0},{8,4},{12,8},{14,12},{10,14},{6,10},{2,6},{1,3},{5,1},... | collective-permute-start | bytes 688136 | tf_op jit(solution)/shard_map/ppermute | solution.py:206
  43.0 7.7 %collective-permute-start.6 = (bf16[16,7296]{1,0:T(8,128)(2,1)S(1)}, bf16[16,7296]{1,0:T(8,128)(2,1)S(1)}, u32[]{:S(2)}, u32[]{:S(2)}) collective-permute-start(bf16[16,7296]{1,0:T(8,128)(2,1)S(1)} %collective-permute-done.4.refs_5_.refs_13_), channel_id=1, source_target_pairs={{0,4},{4,8},{8,12},{12,14},{14,10},{10,6},{6,2},{2,0},{1,5},{5,9},... | collective-permute-start | bytes 700424 | tf_op jit(solution)/shard_map/ppermute | solution.py:203
  53.9 9.2 %collective-permute-start.23 = (bf16[16,7168]{1,0:T(8,128)(2,1)S(1)}, bf16[16,7168]{1,0:T(8,128)(2,1)S(1)}, u32[]{:S(2)}, u32[]{:S(2)}) collective-permute-start(bf16[16,7168]{1,0:T(8,128)(2,1)S(1)} %convert_element_type.98), channel_id=1, source_target_pairs={{0,4},{4,8},{8,12},{12,14},{14,10},{10,6},{6,2},{2,0},{1,5},{5,9},... | collective-permute-start | bytes 688136 | tf_op jit(solution)/shard_map/ppermute | solution.py:203
  54.8 8.8 %collective-permute-start.26 = (bf16[16,7168]{1,0:T(8,128)(2,1)S(1)}, bf16[16,7168]{1,0:T(8,128)(2,1)S(1)}, u32[]{:S(2)}, u32[]{:S(2)}) collective-permute-start(bf16[16,7168]{1,0:T(8,128)(2,1)S(1)} %get-tuple-element.37), channel_id=1, source_target_pairs={{0,2},{4,0},{8,4},{12,8},{14,12},{10,14},{6,10},{2,6},{1,3},{5,1},... | collective-permute-start | bytes 688136 | tf_op jit(solution)/shard_map/ppermute | solution.py:206
  59.9 8.6 %collective-permute-start.9 = (bf16[16,7168]{1,0:T(8,128)(2,1)S(1)}, bf16[16,7168]{1,0:T(8,128)(2,1)S(1)}, u32[]{:S(2)}, u32[]{:S(2)}) collective-permute-start(bf16[16,7168]{1,0:T(8,128)(2,1)S(1)} %get-tuple-element.25), channel_id=1, source_target_pairs={{0,4},{4,8},{8,12},{12,14},{14,10},{10,6},{6,2},{2,0},{1,5},{5,9},... | collective-permute-start | bytes 688136 | tf_op jit(solution)/shard_map/ppermute | solution.py:203
  60.3 8.6 %collective-permute-start.13 = (bf16[16,7168]{1,0:T(8,128)(2,1)S(1)}, bf16[16,7168]{1,0:T(8,128)(2,1)S(1)}, u32[]{:S(2)}, u32[]{:S(2)}) collective-permute-start(bf16[16,7168]{1,0:T(8,128)(2,1)S(1)} %convert_element_type.91), channel_id=1, source_target_pairs={{0,2},{4,0},{8,4},{12,8},{14,12},{10,14},{6,10},{2,6},{1,3},{5,1},... | collective-permute-start | bytes 688136 | tf_op jit(solution)/shard_map/ppermute | solution.py:206
  63.1 9.1 %collective-permute-start.24 = (bf16[16,7168]{1,0:T(8,128)(2,1)S(1)}, bf16[16,7168]{1,0:T(8,128)(2,1)S(1)}, u32[]{:S(2)}, u32[]{:S(2)}) collective-permute-start(bf16[16,7168]{1,0:T(8,128)(2,1)S(1)} %add_convert_fusion.5), channel_id=1, source_target_pairs={{0,4},{4,8},{8,12},{12,14},{14,10},{10,6},{6,2},{2,0},{1,5},{5,9},... | collective-permute-start | bytes 688136 | tf_op jit(solution)/shard_map/ppermute | solution.py:203
  63.6 9.3 %collective-permute-start.27 = (bf16[16,7168]{1,0:T(8,128)(2,1)S(1)}, bf16[16,7168]{1,0:T(8,128)(2,1)S(1)}, u32[]{:S(2)}, u32[]{:S(2)}) collective-permute-start(bf16[16,7168]{1,0:T(8,128)(2,1)S(1)} %add_convert_fusion.3), channel_id=1, source_target_pairs={{0,2},{4,0},{8,4},{12,8},{14,12},{10,14},{6,10},{2,6},{1,3},{5,1},... | collective-permute-start | bytes 688136 | tf_op jit(solution)/shard_map/ppermute | solution.py:206
  68.6 7.0 %collective-permute-start.10 = (bf16[16,7168]{1,0:T(8,128)(2,1)S(1)}, bf16[16,7168]{1,0:T(8,128)(2,1)S(1)}, u32[]{:S(2)}, u32[]{:S(2)}) collective-permute-start(bf16[16,7168]{1,0:T(8,128)(2,1)S(1)} %add_convert_fusion.11), channel_id=1, source_target_pairs={{0,4},{4,8},{8,12},{12,14},{14,10},{10,6},{6,2},{2,0},{1,5},{5,9},... | collective-permute-start | bytes 688136 | tf_op jit(solution)/shard_map/ppermute | solution.py:203
  68.9 7.0 %collective-permute-start.14 = (bf16[16,7168]{1,0:T(8,128)(2,1)S(1)}, bf16[16,7168]{1,0:T(8,128)(2,1)S(1)}, u32[]{:S(2)}, u32[]{:S(2)}) collective-permute-start(bf16[16,7168]{1,0:T(8,128)(2,1)S(1)} %add_convert_fusion.8), channel_id=1, source_target_pairs={{0,2},{4,0},{8,4},{12,8},{14,12},{10,14},{6,10},{2,6},{1,3},{5,1},... | collective-permute-start | bytes 688136 | tf_op jit(solution)/shard_map/ppermute | solution.py:206
  72.3 16.9 %collective-permute-start.25 = (bf16[16,7168]{1,0:T(8,128)(2,1)S(1)}, bf16[16,7168]{1,0:T(8,128)(2,1)S(1)}, u32[]{:S(2)}, u32[]{:S(2)}) collective-permute-start(bf16[16,7168]{1,0:T(8,128)(2,1)S(1)} %add_convert_fusion.4), channel_id=1, source_target_pairs={{0,4},{4,8},{8,12},{12,14},{14,10},{10,6},{6,2},{2,0},{1,5},{5,9},... | collective-permute-start | bytes 688136 | tf_op jit(solution)/shard_map/ppermute | solution.py:203
  73.0 9.8 %collective-permute-start.28 = (bf16[16,7168]{1,0:T(8,128)(2,1)S(1)}, bf16[16,7168]{1,0:T(8,128)(2,1)S(1)}, u32[]{:S(2)}, u32[]{:S(2)}) collective-permute-start(bf16[16,7168]{1,0:T(8,128)(2,1)S(1)} %add_convert_fusion.2), channel_id=1, source_target_pairs={{0,2},{4,0},{8,4},{12,8},{14,12},{10,14},{6,10},{2,6},{1,3},{5,1},... | collective-permute-start | bytes 688136 | tf_op jit(solution)/shard_map/ppermute | solution.py:206
  75.6 6.6 %collective-permute-start.11 = (bf16[16,7168]{1,0:T(8,128)(2,1)S(1)}, bf16[16,7168]{1,0:T(8,128)(2,1)S(1)}, u32[]{:S(2)}, u32[]{:S(2)}) collective-permute-start(bf16[16,7168]{1,0:T(8,128)(2,1)S(1)} %add_convert_fusion.10), channel_id=1, source_target_pairs={{0,4},{4,8},{8,12},{12,14},{14,10},{10,6},{6,2},{2,0},{1,5},{5,9},... | collective-permute-start | bytes 688136 | tf_op jit(solution)/shard_map/ppermute | solution.py:203
  76.0 8.4 %collective-permute-start.15 = (bf16[16,7168]{1,0:T(8,128)(2,1)S(1)}, bf16[16,7168]{1,0:T(8,128)(2,1)S(1)}, u32[]{:S(2)}, u32[]{:S(2)}) collective-permute-start(bf16[16,7168]{1,0:T(8,128)(2,1)S(1)} %add_convert_fusion.7), channel_id=1, source_target_pairs={{0,2},{4,0},{8,4},{12,8},{14,12},{10,14},{6,10},{2,6},{1,3},{5,1},... | collective-permute-start | bytes 688136 | tf_op jit(solution)/shard_map/ppermute | solution.py:206
  82.2 6.1 %collective-permute-start.12 = (bf16[16,7168]{1,0:T(8,128)(2,1)S(1)}, bf16[16,7168]{1,0:T(8,128)(2,1)S(1)}, u32[]{:S(2)}, u32[]{:S(2)}) collective-permute-start(bf16[16,7168]{1,0:T(8,128)(2,1)S(1)} %add_convert_fusion.9), channel_id=1, source_target_pairs={{0,4},{4,8},{8,12},{12,14},{14,10},{10,6},{6,2},{2,0},{1,5},{5,9},... | collective-permute-start | bytes 688136 | tf_op jit(solution)/shard_map/ppermute | solution.py:203
  82.8 6.3 %collective-permute-start.29 = (bf16[16,7168]{1,0:T(8,128)(2,1)S(1)}, bf16[16,7168]{1,0:T(8,128)(2,1)S(1)}, u32[]{:S(2)}, u32[]{:S(2)}) collective-permute-start(bf16[16,7168]{1,0:T(8,128)(2,1)S(1)} %add_convert_fusion.1), channel_id=1, source_target_pairs={{0,2},{4,0},{8,4},{12,8},{14,12},{10,14},{6,10},{2,6},{1,3},{5,1},... | collective-permute-start | bytes 688136 | tf_op jit(solution)/shard_map/ppermute | solution.py:206
